TPU v7x, 8 devices: a whole 2x2x1 slice. The times are simulated.
8 devices in a mesh: cp: 2 (over z, y), fsdp: 4 (over x, core).
Axes of the slice: x: 2, y: 2, z: 1, core: 2. Of those that a mesh axis runs over, the one named last changes fastest.
Arguments:
- act_in: bfloat16 [128, 128, 2048], P('fsdp', 'cp')
- grad_out: bfloat16 [128, 128, 2048], P('fsdp', 'cp')
- positions: int32 [128], P('cp')
- attn_norm: bfloat16 [2048], P(('fsdp', 'cp'))
- w_q: bfloat16 [2048, 32, 64], P(('fsdp', 'cp'))
- w_k: bfloat16 [2048, 4, 64], P(('fsdp', 'cp'))
- w_v: bfloat16 [2048, 4, 64], P(('fsdp', 'cp'))
- w_o: bfloat16 [2048, 2048], P(('fsdp', 'cp'))
- ffn_norm: bfloat16 [2048], P(('fsdp', 'cp'))
- w_gate: bfloat16 [2048, 5632], P(('fsdp', 'cp'))
- w_up: bfloat16 [2048, 5632], P(('fsdp', 'cp'))
- w_down: bfloat16 [5632, 2048], P(('fsdp', 'cp'))
Outputs:
- output 1: bfloat16 [128, 128, 2048], P('fsdp', 'cp')
- output 2: bfloat16 [128, 128, 2048], P('fsdp', 'cp')
- output 3: float32 [2048], P(('fsdp', 'cp'))
- output 4: float32 [2048, 32, 64], P(('fsdp', 'cp'))
- output 5: float32 [2048, 4, 64], P(('fsdp', 'cp'))
- output 6: float32 [2048, 4, 64], P(('fsdp', 'cp'))
- output 7: float32 [2048, 2048], P(('fsdp', 'cp'))
- output 8: float32 [2048], P(('fsdp', 'cp'))
- output 9: float32 [2048, 5632], P(('fsdp', 'cp'))
- output 10: float32 [2048, 5632], P(('fsdp', 'cp'))
- output 11: float32 [5632, 2048], P(('fsdp', 'cp'))
All inputs are finite; a program needn't handle non-finite values.
Results may differ from a plain program's by a relative error of at most 0.0147092.
Values are sent between devices in bfloat16 or wider.
A program may use at most 1 GiB of HBM per device.

v0:
```python
import jax
import jax.numpy as jnp
from jax import lax
from jax.sharding import PartitionSpec as P

NORM_EPS = 1e-5
ROPE_THETA = 500000.0
NEG_INF = -1e30
SHARD_AXES = ("fsdp", "cp")


def contract(form, lhs, rhs):
    return jnp.einsum(form, lhs, rhs, preferred_element_type=jnp.float32)


def rope_tables(positions, head_dim):
    half = head_dim // 2
    inv_freq = jnp.power(ROPE_THETA, -(jnp.arange(half, dtype=jnp.float32) * (2.0 / head_dim)))
    angle = positions.astype(jnp.float32)[:, None] * inv_freq[None, :]
    return jnp.cos(angle), jnp.sin(angle)


def rotate(vals, cos_t, sin_t, sign):
    half = vals.shape[-1] // 2
    table_shape = (cos_t.shape[0],) + (1,) * (vals.ndim - 3) + (half,)
    cos_b = cos_t.reshape(table_shape)
    sin_b = sign * sin_t.reshape(table_shape)
    first = vals[..., :half]
    second = vals[..., half:]
    return jnp.concatenate([first * cos_b - second * sin_b, second * cos_b + first * sin_b], axis=-1)


def norm_fwd(hidden, gain):
    hid32 = hidden.astype(jnp.float32)
    inv_rms = lax.rsqrt(jnp.mean(hid32 * hid32, axis=-1, keepdims=True) + NORM_EPS)
    unit = hid32 * inv_rms
    return (unit * gain.astype(jnp.float32)).astype(jnp.bfloat16), unit, inv_rms


def norm_bwd(d_normed, unit, inv_rms, gain):
    d_unit = d_normed * gain.astype(jnp.float32)
    d_hidden = inv_rms * (d_unit - unit * jnp.mean(d_unit * unit, axis=-1, keepdims=True))
    return d_hidden, jnp.sum(d_normed * unit, axis=(0, 1))


def gather_weight(shard):
    return lax.all_gather(shard, SHARD_AXES, axis=0, tiled=True)


def scatter_grad(local_grad, n_dev):
    return lax.psum_scatter(local_grad, SHARD_AXES, scatter_dimension=0, tiled=True) / n_dev


def solution(mesh):
    n_dev = mesh.shape["fsdp"] * mesh.shape["cp"]
    act_spec = P("fsdp", "cp", None)
    vec_spec = P(SHARD_AXES)
    mat_spec = P(SHARD_AXES, None)
    cube_spec = P(SHARD_AXES, None, None)

    def body(act_in, grad_out, positions, attn_norm, w_q, w_k, w_v, w_o, ffn_norm, w_gate, w_up, w_down):
        batch, seq_len = act_in.shape[0], act_in.shape[1]
        heads, head_dim = w_q.shape[1], w_q.shape[2]
        kv_heads = w_k.shape[1]
        groups = heads // kv_heads
        scale = head_dim ** -0.5
        pos_all = lax.all_gather(positions, "cp", tiled=True)
        cos_t, sin_t = rope_tables(positions, head_dim)
        allowed = pos_all[None, :] <= positions[:, None]

        normed, attn_unit, attn_rms = norm_fwd(act_in, gather_weight(attn_norm))
        query = contract("btd,dhe->bthe", normed, gather_weight(w_q))
        query = rotate(query.reshape(batch, seq_len, kv_heads, groups, head_dim), cos_t, sin_t, 1.0).astype(jnp.bfloat16)
        key_loc = rotate(contract("btd,dke->btke", normed, gather_weight(w_k)), cos_t, sin_t, 1.0).astype(jnp.bfloat16)
        val_loc = contract("btd,dke->btke", normed, gather_weight(w_v)).astype(jnp.bfloat16)
        key_all = lax.all_gather(key_loc, "cp", axis=1, tiled=True)
        val_all = lax.all_gather(val_loc, "cp", axis=1, tiled=True)
        scores = jnp.where(allowed, contract("bqkgd,bskd->bkgqs", query, key_all) * scale, NEG_INF)
        attn_prob = jnp.exp(scores - jnp.max(scores, axis=-1, keepdims=True))
        attn_prob = attn_prob / jnp.sum(attn_prob, axis=-1, keepdims=True)
        prob_half = attn_prob.astype(jnp.bfloat16)
        attn_ctx = contract("bkgqs,bskd->bqkgd", prob_half, val_all).astype(jnp.bfloat16)
        attn_ctx = attn_ctx.reshape(batch, seq_len, heads * head_dim)
        resid = (act_in.astype(jnp.float32) + contract("btn,nd->btd", attn_ctx, gather_weight(w_o))).astype(jnp.bfloat16)
        normed2, ffn_unit, ffn_rms = norm_fwd(resid, gather_weight(ffn_norm))
        gate_pre = contract("btd,df->btf", normed2, gather_weight(w_gate))
        up_pre = contract("btd,df->btf", normed2, gather_weight(w_up))
        gate_sig = jax.nn.sigmoid(gate_pre)
        gate_act = gate_pre * gate_sig
        hidden = (gate_act * up_pre).astype(jnp.bfloat16)
        act_out = (resid.astype(jnp.float32) + contract("btf,fd->btd", hidden, gather_weight(w_down))).astype(jnp.bfloat16)

        act_out, shards = lax.optimization_barrier((act_out, (attn_norm, w_q, w_k, w_v, w_o, ffn_norm, w_gate, w_up, w_down)))
        attn_norm2, w_q2, w_k2, w_v2, w_o2, ffn_norm2, w_gate2, w_up2, w_down2 = shards

        grad_f32 = grad_out.astype(jnp.float32)
        grad_down = contract("btf,btd->fd", hidden, grad_out)
        d_hidden = contract("btd,fd->btf", grad_out, gather_weight(w_down2))
        d_gate = (d_hidden * up_pre * gate_sig * (1.0 + gate_pre * (1.0 - gate_sig))).astype(jnp.bfloat16)
        d_up = (d_hidden * gate_act).astype(jnp.bfloat16)
        grad_gate = contract("btd,btf->df", normed2, d_gate)
        grad_up = contract("btd,btf->df", normed2, d_up)
        d_normed2 = contract("btf,df->btd", d_gate, gather_weight(w_gate2)) + contract("btf,df->btd", d_up, gather_weight(w_up2))
        d_resid, grad_ffn = norm_bwd(d_normed2, ffn_unit, ffn_rms, gather_weight(ffn_norm2))
        d_resid = d_resid + grad_f32
        d_resid_half = d_resid.astype(jnp.bfloat16)
        grad_o = contract("btn,btd->nd", attn_ctx, d_resid_half)
        d_ctx = contract("btd,nd->btn", d_resid_half, gather_weight(w_o2)).astype(jnp.bfloat16)
        d_ctx = d_ctx.reshape(batch, seq_len, kv_heads, groups, head_dim)
        d_prob = contract("bqkgd,bskd->bkgqs", d_ctx, val_all)
        d_val_all = contract("bkgqs,bqkgd->bskd", prob_half, d_ctx)
        d_score = (attn_prob * (d_prob - jnp.sum(attn_prob * d_prob, axis=-1, keepdims=True)) * scale).astype(jnp.bfloat16)
        d_query = contract("bkgqs,bskd->bqkgd", d_score, key_all)
        d_key_all = contract("bkgqs,bqkgd->bskd", d_score, query)
        d_key = lax.psum_scatter(d_key_all, "cp", scatter_dimension=1, tiled=True)
        d_val = lax.psum_scatter(d_val_all, "cp", scatter_dimension=1, tiled=True).astype(jnp.bfloat16)
        d_query = rotate(d_query, cos_t, sin_t, -1.0).astype(jnp.bfloat16).reshape(batch, seq_len, heads, head_dim)
        d_key = rotate(d_key, cos_t, sin_t, -1.0).astype(jnp.bfloat16)
        grad_q = contract("btd,bthe->dhe", normed, d_query)
        grad_k = contract("btd,btke->dke", normed, d_key)
        grad_v = contract("btd,btke->dke", normed, d_val)
        d_normed = (contract("bthe,dhe->btd", d_query, gather_weight(w_q2))
                    + contract("btke,dke->btd", d_key, gather_weight(w_k2))
                    + contract("btke,dke->btd", d_val, gather_weight(w_v2)))
        d_input, grad_attn = norm_bwd(d_normed, attn_unit, attn_rms, gather_weight(attn_norm2))
        grad_in = (d_resid + d_input).astype(jnp.bfloat16)
        return (act_out, grad_in, scatter_grad(grad_attn, n_dev), scatter_grad(grad_q, n_dev), scatter_grad(grad_k, n_dev), scatter_grad(grad_v, n_dev), scatter_grad(grad_o, n_dev), scatter_grad(grad_ffn, n_dev), scatter_grad(grad_gate, n_dev), scatter_grad(grad_up, n_dev), scatter_grad(grad_down, n_dev))

    in_specs = (act_spec, act_spec, P("cp"), vec_spec, cube_spec, cube_spec, cube_spec, mat_spec, vec_spec, mat_spec, mat_spec, mat_spec)
    out_specs = (act_spec, act_spec, vec_spec, cube_spec, cube_spec, cube_spec, mat_spec, vec_spec, mat_spec, mat_spec, mat_spec)
    return jax.shard_map(body, mesh=mesh, in_specs=in_specs, out_specs=out_specs, check_vma=False)
```

profile of v0, /device:TPU:0, one launch (start us, length us, event | category | flops | bytes accessed | tf_op | source)
XLA Modules:
  0.0 3103.6 jit_solution(8193889463472305423)
XLA Ops:
  79.0 27.5 all-gather.27.cloned.1.call-done
  112.0 46.2 %all-gather.29.cloned.1.call-done = bf16[2048,32,64]{0,2,1:T(8,128)(2,1)} async-done(((bf16[256,32,64]{0,2,1:T(8,128)(2,1)}), bf16[2048,32,64]{0,2,1:T(8,128)(2,1)}) %all-gather.29.cloned.1.call-update) | async-done | bytes 8388624 | tf_op jit(solution)/shard_map/all_gather | solution.py:47
  158.2 42.4 %fusion.62 = f32[32,64,32,64]{1,3,2,0:T(8,128)} fusion(bf16[2048,32,64]{0,2,1:T(8,128)(2,1)} %all-gather.29.cloned.1.call-done, bf16[32,64,2048]{2,1,0:T(8,128)(2,1)} %param.12, f32[2048]{0:T(1024)S(1)} %bitcast.259, f32[32,64]{1,0:T(8,128)S(1)} %add_rsqrt_fusion.1), kind=kOutput, calls=%fused_computation.90 | convolution fusion | flops 17196646400 | bytes 33570816 | tf_op jit(solution)/shard_map/btd,dhe->bthe/dot_general | solution.py:13
  268.9 32.9 %subtract_convert_fusion.1 = (bf16[32,64,4,8,32]{4,1,3,2,0:T(8,128)(2,1)}, bf16[32,64,4,8,32]{4,1,3,2,0:T(8,128)(2,1)}) fusion(f32[32,64,4,8,32]{4,1,3,2,0:T(8,128)} %copy.93, f32[32,64,4,8,32]{4,1,3,2,0:T(8,128)} %copy.92, f32[64,32]{1,0:T(8,128)S(1)} %copy.45, f32[64,32]{1,0:T(8,128)S(1)} %copy.43), kind=kLoop, calls=%fused_computation.21 | loop fusion | flops 16777216 | bytes 25182208 | tf_op jit(solution)/shard_map/convert.6
  301.8 31.0 fusion.118
  332.8 25.1 convolution_convert_fusion
  358.0 28.3 fusion.46
  386.4 58.7 %fusion.29 = f32[32,64,5632]{2,1,0:T(8,128)} fusion(bf16[2048,5632]{1,0:T(8,128)(2,1)} %all-gather.33.cloned.1.call-done, bf16[32,64,2048]{2,1,0:T(8,128)(2,1)} %get-tuple-element.57, f32[2048]{0:T(1024)S(1)} %bitcast.263, f32[32,64]{1,0:T(8,128)S(1)} %add_rsqrt_fusion), kind=kOutput, calls=%fused_computation.50 | convolution fusion | flops 47261417472 | bytes 77611008 | tf_op jit(solution)/shard_map/btd,df->btf/dot_general | solution.py:13
  445.1 44.5 %all-gather.35.cloned.1.call-done = bf16[2048,5632]{1,0:T(8,128)(2,1)} async-done(((bf16[256,5632]{1,0:T(8,128)(2,1)}), bf16[2048,5632]{1,0:T(8,128)(2,1)}) %all-gather.35.cloned.1.call-update) | async-done | bytes 23068688 | tf_op jit(solution)/shard_map/all_gather | solution.py:47
  489.6 64.1 %multiply_convert_fusion = (bf16[32,64,5632]{2,1,0:T(8,128)(2,1)}, f32[32,64,5632]{2,1,0:T(8,128)}) fusion(f32[32,64,5632]{2,1,0:T(8,128)} %fusion.29, bf16[2048,5632]{1,0:T(8,128)(2,1)} %all-gather.35.cloned.1.call-done, bf16[32,64,2048]{2,1,0:T(8,128)(2,1)} %get-tuple-element.57, f32[2048]{0:T(1024)S(1)} %bitcast.264, f32[32,64]{1,0:T(8,128)S(1)} %add_rsqrt_fusion), kind=kOutput, calls=%fused_computation.8 | convolution fusion | flops 47330623488 | bytes 146817024 | tf_op jit(solution)/shard_map/btd,df->btf/dot_general | solution.py:13
  553.7 48.5 %all-gather.37.cloned.1.call-done = bf16[5632,2048]{1,0:T(8,128)(2,1)} async-done(((bf16[704,2048]{1,0:T(8,128)(2,1)}), bf16[5632,2048]{1,0:T(8,128)(2,1)}) %all-gather.37.cloned.1.call-update) | async-done | bytes 23068688 | tf_op jit(solution)/shard_map/all_gather | solution.py:47
  602.2 60.3 %fusion.47 = bf16[32,64,2048]{2,1,0:T(8,128)(2,1)} fusion(bf16[32,64,2048]{2,1,0:T(8,128)(2,1)} %get-tuple-element.57, bf16[32,64,5632]{2,1,0:T(8,128)(2,1)} %get-tuple-element.58, bf16[5632,2048]{1,0:T(8,128)(2,1)} %all-gather.37.cloned.1.call-done), kind=kOutput, calls=%fused_computation.68 | convolution fusion | flops 47257223168 | bytes 62914560 | tf_op jit(solution)/shard_map/btf,fd->btd/dot_general | solution.py:13
  675.3 98.1 %all-gather.39.cloned.1.call-done = bf16[5632,2048]{1,0:T(8,128)(2,1)} async-done(((bf16[704,2048]{1,0:T(8,128)(2,1)}), bf16[5632,2048]{1,0:T(8,128)(2,1)}) %all-gather.39.cloned.1.call-update) | async-done | bytes 23068688 | tf_op jit(solution)/shard_map/all_gather | solution.py:47
  773.4 85.9 %fusion.4 = (bf16[32,64,5632]{2,1,0:T(8,128)(2,1)}, bf16[32,64,5632]{2,1,0:T(8,128)(2,1)}) fusion(f32[32,64,5632]{2,1,0:T(8,128)} %get-tuple-element.59, f32[32,64,5632]{2,1,0:T(8,128)} %fusion.29, bf16[32,64,2048]{2,1,0:T(8,128)(2,1)} %param.13, bf16[5632,2048]{1,0:T(8,128)(2,1)} %all-gather.39.cloned.1.call-done), kind=kOutput, calls=%fused_computation.6 | convolution fusion | flops 47394586624 | bytes 169869312 | tf_op jit(solution)/shard_map/btd,fd->btf/dot_general | solution.py:13
  859.3 26.7 all-gather.43.cloned.1.call-done
  886.0 60.3 %fusion.19 = f32[32,64,2048]{2,1,0:T(8,128)} fusion(bf16[32,64,5632]{2,1,0:T(8,128)(2,1)} %get-tuple-element.38, bf16[2048,5632]{1,0:T(8,128)(2,1)} %all-gather.43.cloned.1.call-done), kind=kOutput, calls=%fused_computation.40 | convolution fusion | flops 47244640256 | bytes 62914560 | tf_op jit(solution)/shard_map/btf,df->btd/dot_general | solution.py:13
  946.4 52.1 %all-gather.41.cloned.1.call-done = bf16[2048,5632]{1,0:T(8,128)(2,1)} async-done(((bf16[256,5632]{1,0:T(8,128)(2,1)}), bf16[2048,5632]{1,0:T(8,128)(2,1)}) %all-gather.41.cloned.1.call-update) | async-done | bytes 23068688 | tf_op jit(solution)/shard_map/all_gather | solution.py:47
  998.5 68.7 %fusion.45 = (f32[2048]{0:T(1024)}, f32[32,64]{1,0:T(8,128)S(1)}, f32[32,64,2048]{2,1,0:T(8,128)}) fusion(bf16[32,64,2048]{2,1,0:T(8,128)(2,1)} %get-tuple-element.57, f32[32,64]{1,0:T(8,128)S(1)} %copy-done.17, f32[2048]{0:T(1024)S(1)} %bitcast.255, f32[32,64,2048]{2,1,0:T(8,128)} %fusion.19, bf16[32,64,5632]{2,1,0:T(8,128)(2,1)} %get-tuple-element.37, ...), kind=kOutput, calls=%fused_computation.66 | convolution fusion | flops 47278194688 | bytes 88113152 | tf_op jit(solution)/shard_map/btf,df->btd/dot_general | solution.py:13
  1084.2 25.0 fusion.72
  1147.4 392.6 %fusion.91 = f32[32,128,4,64]{1,3,2,0:T(8,128)} fusion(f32[32,4,128,64,8]{2,3,4,1,0:T(8,128)} %fusion.77, bf16[32,64,4,8,32]{4,1,3,2,0:T(8,128)(2,1)} %get-tuple-element.40, bf16[32,64,4,8,32]{4,1,3,2,0:T(8,128)(2,1)} %get-tuple-element.39, f32[32,4,8,64,128]{4,3,2,1,0:T(8,128)} %get-tuple-element.55, f32[32,4,8,64]{3,2,1,0:T(8,128)S(1)} %copy-done.32), kind=kOutput, calls=%fused_computation.110 | convolution fusion | flops 1149304960 | bytes 79953920 | tf_op jit(solution)/shard_map/bkgqs,bqkgd->bskd/dot_general | solution.py:13
  1599.3 376.1 %fusion.54 = f32[32,64,4,8,64]{4,1,3,2,0:T(8,128)} fusion(bf16[32,128,4,64,1]{1,3,4,2,0:T(8,128)(2,1)S(1)} %copy-done.6, f32[32,4,128,64,8]{2,3,4,1,0:T(8,128)} %fusion.77, f32[32,4,8,64,128]{4,3,2,1,0:T(8,128)} %get-tuple-element.55, f32[32,4,8,64]{3,2,1,0:T(8,128)S(1)} %copy-done.32), kind=kOutput, calls=%fused_computation.80 | convolution fusion | flops 1132527744 | bytes 86245376 | tf_op jit(solution)/shard_map/bkgqs,bskd->bqkgd/dot_general | solution.py:13
  2010.1 33.7 %subtract_convert_fusion = (bf16[32,64,4,8,32]{4,1,3,2,0:T(8,128)(2,1)}, bf16[32,64,4,8,32]{4,1,3,2,0:T(8,128)(2,1)}) fusion(f32[32,64,4,8,64]{4,1,3,2,0:T(8,128)} %fusion.54, f32[64,32]{1,0:T(8,128)S(1)} %copy-done.15, f32[64,32]{1,0:T(8,128)S(1)} %copy-done.8), kind=kLoop, calls=%fused_computation.18 | loop fusion | flops 16777216 | bytes 25182208 | tf_op jit(solution)/shard_map/convert.5
  2060.2 30.8 convolution_bitcast_fusion.4
  2091.1 27.7 convolution_bitcast_fusion.3
  2118.8 58.6 %convolution_bitcast_fusion = f32[5632,2048]{1,0:T(8,128)} fusion(bf16[32,64,5632]{2,1,0:T(8,128)(2,1)} %get-tuple-element.58, bf16[32,64,2048]{2,1,0:T(8,128)(2,1)} %param.13), kind=kOutput, calls=%fused_computation.22 | convolution fusion | flops 47244640256 | bytes 77594624 | tf_op jit(solution)/shard_map/btf,btd->fd/dot_general | solution.py:13
  2178.1 60.3 %convolution_bitcast_fusion.1 = f32[2048,5632]{1,0:T(8,128)} fusion(bf16[32,64,5632]{2,1,0:T(8,128)(2,1)} %get-tuple-element.38, bf16[32,64,2048]{2,1,0:T(8,128)(2,1)} %get-tuple-element.57, f32[2048]{0:T(1024)S(1)} %bitcast.265, f32[32,64]{1,0:T(8,128)S(1)} %copy-done.18), kind=kOutput, calls=%fused_computation.23 | convolution fusion | flops 47261417472 | bytes 77611008 | tf_op jit(solution)/shard_map/btd,btf->df/dot_general | solution.py:13
  2238.5 60.7 %convolution_bitcast_fusion.2 = f32[2048,5632]{1,0:T(8,128)} fusion(bf16[32,64,5632]{2,1,0:T(8,128)(2,1)} %get-tuple-element.37, bf16[32,64,2048]{2,1,0:T(8,128)(2,1)} %get-tuple-element.57, f32[2048]{0:T(1024)S(1)} %bitcast.266, f32[32,64]{1,0:T(8,128)S(1)} %copy-done.18), kind=kOutput, calls=%fused_computation.24 | convolution fusion | flops 47261417472 | bytes 77611008 | tf_op jit(solution)/shard_map/btd,btf->df/dot_general | solution.py:13
  2312.1 33.1 %fusion.56 = f32[32,64,2048,1]{2,1,3,0:T(8,128)} fusion(bf16[2048,32,64]{0,2,1:T(8,128)(2,1)} %all-gather.47.cloned.1.call-done, bf16[32,64,32,32]{3,1,2,0:T(8,128)(2,1)} %bitcast.250, bf16[32,64,32,32]{3,1,2,0:T(8,128)(2,1)} %bitcast.248), kind=kOutput, calls=%fused_computation.84 | convolution fusion | flops 17196646400 | bytes 33554432 | tf_op jit(solution)/shard_map/bthe,dhe->btd/dot_general | solution.py:13
  2377.0 23.2 all-reduce.3
  2428.3 145.7 %reduce-scatter.26.cloned.1.call-done = f32[704,2048]{1,0:T(8,128)} async-done(((f32[5632,2048]{1,0:T(8,128)}), f32[704,2048]{1,0:T(8,128)}) %reduce-scatter.26.cloned.1.call-update) | async-done | bytes 5767184 | tf_op jit(solution)/shard_map/reduce_scatter | solution.py:51
  2580.2 252.4 %reduce-scatter.24.cloned.1.call-done = f32[256,5632]{1,0:T(8,128)} async-done(((f32[2048,5632]{1,0:T(8,128)}), f32[256,5632]{1,0:T(8,128)}) %reduce-scatter.24.cloned.1.call-update) | async-done | bytes 5767184 | tf_op jit(solution)/shard_map/reduce_scatter | solution.py:51
  2838.2 253.1 %reduce-scatter.22.cloned.1.call-done = f32[256,5632]{1,0:T(8,128)} async-done(((f32[2048,5632]{1,0:T(8,128)}), f32[256,5632]{1,0:T(8,128)}) %reduce-scatter.22.cloned.1.call-update) | async-done | bytes 5767184 | tf_op jit(solution)/shard_map/reduce_scatter | solution.py:51
  (197 shorter events, 413.0 us)
Async XLA Ops:
  7.2 23.2 all-gather.25.cloned.1.call-start
  7.9 42.0 %all-gather.21.cloned.1.call-start = ((), (), s32[]{:S(2)}) async-start(), calls=%async_computation.9 | async-start | bytes 1179648 | tf_op jit(solution)/shard_map/all_gather | solution.py:47
  8.7 97.8 %all-gather.27.cloned.1.call-start = ((), (), s32[]{:S(2)}) async-start(), calls=%async_computation.12 | async-start | bytes 6291456 | tf_op jit(solution)/shard_map/all_gather | solution.py:76
  13.8 144.4 %copy-start.12 = (f32[32,64]{1,0:T(8,128)}, f32[32,64]{1,0:T(8,128)S(1)}, u32[]{:S(2)}) copy-start(f32[32,64]{1,0:T(8,128)S(1)} %add_rsqrt_fusion.1) | copy-start | bytes 24580
  28.1 130.1 %copy-start.20 = (f32[8,1,256]{2,1,0:T(1,128)}, f32[8,1,256]{2,1,0:T(1,128)S(1)}, u32[]{:S(2)}) copy-start(f32[8,1,256]{2,1,0:T(1,128)S(1)} %convert_element_type.103) | copy-start | bytes 24580
  42.8 115.4 %all-gather.29.cloned.1.call-start = ((), (), s32[]{:S(2)}) async-start(), calls=%async_computation.13 | async-start | bytes 9437184 | tf_op jit(solution)/shard_map/all_gather | solution.py:47
  43.4 289.4 %all-gather.23.cloned.1.call-start = ((), (), s32[]{:S(2)}) async-start(), calls=%async_computation.10 | async-start | bytes 6291456 | tf_op jit(solution)/shard_map/all_gather | solution.py:77
  58.2 299.8 %all-gather.31.cloned.1.call-start = ((), (), s32[]{:S(2)}) async-start(), calls=%async_computation.14 | async-start | bytes 9437184 | tf_op jit(solution)/shard_map/all_gather | solution.py:47
  58.8 327.5 %all-gather.33.cloned.1.call-start = ((), (), s32[]{:S(2)}) async-start(), calls=%async_computation.15 | async-start | bytes 25952256 | tf_op jit(solution)/shard_map/all_gather | solution.py:47
  59.5 430.0 %all-gather.35.cloned.1.call-start = ((), (), s32[]{:S(2)}) async-start(), calls=%async_computation.16 | async-start | bytes 25952256 | tf_op jit(solution)/shard_map/all_gather | solution.py:47
  60.3 541.9 %all-gather.37.cloned.1.call-start = ((), (), s32[]{:S(2)}) async-start(), calls=%async_computation.17 | async-start | bytes 25952256 | tf_op jit(solution)/shard_map/all_gather | solution.py:47
  61.0 712.4 %all-gather.39.cloned.1.call-start = ((), (), s32[]{:S(2)}) async-start(), calls=%async_computation.18 | async-start | bytes 25952256 | tf_op jit(solution)/shard_map/all_gather | solution.py:47
  61.2 207.7 %copy-start.7 = (f32[64,32]{1,0:T(8,128)}, f32[64,32]{1,0:T(8,128)S(1)}, u32[]{:S(2)}) copy-start(f32[64,32]{1,0:T(8,128)S(1)} %copy.43) | copy-start | bytes 24580
  112.0 189.8 %copy-start.5 = (bf16[32,128,4,64,1]{1,3,4,2,0:T(8,128)(2,1)}, bf16[32,128,4,64,1]{1,3,4,2,0:T(8,128)(2,1)S(1)}, u32[]{:S(2)}) copy-start(bf16[32,128,4,64,1]{1,3,4,2,0:T(8,128)(2,1)S(1)} %copy.66) | copy-start | bytes 6291460
  386.3 103.2 %copy-start.16 = (f32[32,64]{1,0:T(8,128)}, f32[32,64]{1,0:T(8,128)S(1)}, u32[]{:S(2)}) copy-start(f32[32,64]{1,0:T(8,128)S(1)} %add_rsqrt_fusion) | copy-start | bytes 24580
  662.5 223.5 %all-gather.43.cloned.1.call-start = ((), (), s32[]{:S(2)}) async-start(), calls=%async_computation.20 | async-start | bytes 25952256 | tf_op jit(solution)/shard_map/all_gather | solution.py:47
  663.2 335.2 %all-gather.41.cloned.1.call-start = ((), (), s32[]{:S(2)}) async-start(), calls=%async_computation.19 | async-start | bytes 25952256 | tf_op jit(solution)/shard_map/all_gather | solution.py:47
  663.8 420.4 %all-gather.45.cloned.1.call-start = ((), (), s32[]{:S(2)}) async-start(), calls=%async_computation.21 | async-start | bytes 9437184 | tf_op jit(solution)/shard_map/all_gather | solution.py:47
  675.3 1300.1 %reduce-scatter.28.cloned.1.call-start = ((), (), s32[]{:S(2)}) async-start(), calls=%async_computation.32 | async-start | bytes 6291456
  886.0 112.5 %copy-start.17 = (f32[32,64]{1,0:T(8,128)S(1)}, f32[32,64]{1,0:T(8,128)}, u32[]{:S(2)}) copy-start(f32[32,64]{1,0:T(8,128)} %copy-done.16) | copy-start | bytes 24580
  886.0 112.5 %copy-start.19 = (f32[8,1,256]{2,1,0:T(1,128)S(1)}, f32[8,1,256]{2,1,0:T(1,128)}, u32[]{:S(2)}) copy-start(f32[8,1,256]{2,1,0:T(1,128)} %convert_element_type.105) | copy-start | bytes 24580
  1558.2 485.6 %reduce-scatter.30.cloned.1.call-start = ((), (), s32[]{:S(2)}) async-start(), calls=%async_computation.33 | async-start | bytes 6291456
  1597.3 714.7 %all-gather.47.cloned.1.call-start = ((), (), s32[]{:S(2)}) async-start(), calls=%async_computation.22 | async-start | bytes 9437184 | tf_op jit(solution)/shard_map/all_gather | solution.py:47
  1597.9 747.3 %all-gather.49.cloned.1.call-start = ((), (), s32[]{:S(2)}) async-start(), calls=%async_computation.23 | async-start | bytes 1179648 | tf_op jit(solution)/shard_map/all_gather | solution.py:47
  1598.5 756.7 %all-gather.51.cloned.1.call-start = ((), (), s32[]{:S(2)}) async-start(), calls=%async_computation.24 | async-start | bytes 1179648 | tf_op jit(solution)/shard_map/all_gather | solution.py:47
  1599.3 819.4 %reduce-scatter.16.cloned.1.call-start = ((), (), s32[]{:S(2)}) async-start(), calls=%async_computation.26 | async-start | bytes 2359296 | tf_op jit(solution)/shard_map/reduce_scatter | solution.py:51
  2010.0 410.4 %reduce-scatter.18.cloned.1.call-start = ((), (), s32[]{:S(2)}) async-start(), calls=%async_computation.27 | async-start | bytes 2359296 | tf_op jit(solution)/shard_map/reduce_scatter | solution.py:51
  2060.1 361.9 %reduce-scatter.14.cloned.1.call-start = ((), (), s32[]{:S(2)}) async-start(), calls=%async_computation.25 | async-start | bytes 18874368 | tf_op jit(solution)/shard_map/reduce_scatter | solution.py:51
  2091.0 334.2 %reduce-scatter.20.cloned.1.call-start = ((), (), s32[]{:S(2)}) async-start(), calls=%async_computation.28 | async-start | bytes 18874368 | tf_op jit(solution)/shard_map/reduce_scatter | solution.py:51
  2118.8 455.3 %reduce-scatter.26.cloned.1.call-start = ((), (), s32[]{:S(2)}) async-start(), calls=%async_computation.31 | async-start | bytes 51904512 | tf_op jit(solution)/shard_map/reduce_scatter | solution.py:51
  2177.4 655.2 %reduce-scatter.24.cloned.1.call-start = ((), (), s32[]{:S(2)}) async-start(), calls=%async_computation.30 | async-start | bytes 51904512 | tf_op jit(solution)/shard_map/reduce_scatter | solution.py:51
  2238.5 852.9 %reduce-scatter.22.cloned.1.call-start = ((), (), s32[]{:S(2)}) async-start(), calls=%async_computation.29 | async-start | bytes 51904512 | tf_op jit(solution)/shard_map/reduce_scatter | solution.py:51
  (26 other events, 439.8 us)
Sparse Core Ops, SparseCore 0:
  9.8 20.5 all-gather.24
  32.2 17.6 all-gather.20
  52.0 54.4 all-gather.26
  108.2 49.9 all-gather.28
  160.1 54.1 all-gather.22
  216.0 48.3 all-gather.30
  266.2 110.7 all-gather.32
  378.8 110.7 all-gather.34
  491.4 110.7 all-gather.36
  662.6 110.7 all-gather.38
  775.2 110.7 all-gather.42
  887.7 110.7 all-gather.40
  1000.3 48.3 all-gather.44
  1558.3 51.4 reduce-scatter.27
  1612.5 51.5 reduce-scatter.29
  1665.8 50.3 all-gather.46
  1717.8 18.0 all-gather.48
  1737.6 17.8 all-gather.50
  2010.1 32.5 reduce-scatter.15
  2060.3 32.5 reduce-scatter.17
  2096.4 106.9 reduce-scatter.13
  2206.8 107.1 reduce-scatter.19
  2317.5 256.4 reduce-scatter.25
  2577.5 255.0 reduce-scatter.23
  2836.2 255.1 reduce-scatter.21
where the time goes:
time: 3110 us; the launch traced here: 3100 us
  matrix products  1700 us (55%)
  waiting for transfers between devices  1010 us (32%)
  local copies, waits for them, and re-layouts  168 us (5%)
  other arithmetic  140 us (5%)
  blocking collectives  74 us (2%)
    dot_general x26, matrix products, contract(): return jnp.einsum(form, lhs, rhs, preferred_element_type=jnp.float32)  1660 us
    reduce_scatter x7, waiting for transfers between devices, scatter_grad(): lax.psum_scatter(local_grad, SHARD_AXES, scatter_dimension=0, tiled=True)  651 us
    all_gather x14, waiting for transfers between devices, gather_weight(): return lax.all_gather(shard, SHARD_AXES, axis=0, tiled=True)  323 us
    unnamed x85, local copies, waits for them, and re-layouts  111 us
    another operation x4, other arithmetic  69.4 us
  transfers between devices with their start and end apart: 25, of which 12 were waited for; matrix products, arithmetic and copies ran while one was open for 47% of the time, Pallas kernels for 0%

commit v1 on v0

v1 whole, which is shorter than its diff:
```python
import functools

import jax
import jax.numpy as jnp
from jax import lax
from jax.experimental import pallas as pl
from jax.experimental.pallas import tpu as pltpu
from jax.sharding import PartitionSpec as P


NORM_EPS = 1e-5
ROPE_THETA = 500000.0
NEG_INF = -1e30
SHARD_AXES = ("fsdp", "cp")
LANES = 128
HALF_SLAB = 64


def matmul(form, lhs, rhs):
    return jnp.einsum(form, lhs, rhs, preferred_element_type=jnp.float32)


def dims(lhs_dim, rhs_dim):
    return (((lhs_dim,), (rhs_dim,)), ((), ()))


def kdot(lhs, rhs, lhs_dim, rhs_dim):
    return lax.dot_general(lhs, rhs, dims(lhs_dim, rhs_dim), preferred_element_type=jnp.float32)


def lane_of(rows):
    return lax.broadcasted_iota(jnp.int32, (rows, LANES), 1)


def partner_half(vals):
    low = (lane_of(vals.shape[0]) % 64) < 32
    return jnp.where(low, pltpu.roll(vals, LANES - 32, 1), pltpu.roll(vals, 32, 1))


def pair_blocks(slab, odd):
    wide = slab.astype(jnp.float32)
    low = lane_of(wide.shape[0]) < HALF_SLAB
    mine = jnp.where(low, 0.0, wide) if odd else jnp.where(low, wide, 0.0)
    moved = pltpu.roll(mine, HALF_SLAB, 1)
    parts = (moved, mine) if odd else (mine, moved)
    return jnp.concatenate(parts, axis=0).astype(jnp.bfloat16)


def rope_kv_kernel(kv_ref, cos_ref, sin_ref, out_ref):
    reps = kv_ref.shape[0] // cos_ref.shape[0]
    cos_t = jnp.concatenate([cos_ref[...]] * reps, axis=0)
    sin_t = jnp.concatenate([sin_ref[...]] * reps, axis=0)
    for j in range(2):
        cols = slice(j * LANES, (j + 1) * LANES)
        vals = kv_ref[:, cols]
        out_ref[:, cols] = (vals * cos_t + partner_half(vals) * sin_t).astype(jnp.bfloat16)
    out_ref[:, 2 * LANES:] = kv_ref[:, 2 * LANES:].astype(jnp.bfloat16)


def unrope_kv_kernel(own_ref, got_ref, cos_ref, sin_ref, wide_ref, out_ref):
    del wide_ref
    reps = own_ref.shape[0] // cos_ref.shape[0]
    cos_t = jnp.concatenate([cos_ref[...]] * reps, axis=0)
    sin_t = jnp.concatenate([sin_ref[...]] * reps, axis=0)
    for j in range(2):
        cols = slice(j * LANES, (j + 1) * LANES)
        vals = own_ref[:, cols] + got_ref[:, cols]
        out_ref[:, cols] = (vals * cos_t - partner_half(vals) * sin_t).astype(jnp.bfloat16)
    out_ref[:, 2 * LANES:] = (own_ref[:, 2 * LANES:] + got_ref[:, 2 * LANES:]).astype(jnp.bfloat16)


def stack_slabs(ref, group):
    return jnp.concatenate([ref[:, pl.ds((group * 4 + j) * LANES, LANES)] for j in range(4)], axis=0)


def write_slabs(ref, group, vals):
    rows = vals.shape[0] // 4
    for j in range(4):
        ref[:, pl.ds((group * 4 + j) * LANES, LANES)] = vals[j * rows:(j + 1) * rows].astype(ref.dtype)


def kv_pair(kv_ref, kvo_ref, group):
    at = (group // 2) * LANES
    odd = group % 2 == 1
    key = jnp.concatenate([kv_ref[:, at:at + LANES], kvo_ref[:, at:at + LANES]], axis=0)
    at += 2 * LANES
    val = jnp.concatenate([kv_ref[:, at:at + LANES], kvo_ref[:, at:at + LANES]], axis=0)
    return pair_blocks(key, odd), pair_blocks(val, odd)


def softmax_pair(query, key2, mask, scale):
    scores = kdot(query, key2, 1, 1) * scale
    probs = []
    for j in range(2):
        part = jnp.where(mask, scores[:, j * LANES:(j + 1) * LANES], NEG_INF)
        expo = jnp.exp(part - jnp.max(part, axis=1, keepdims=True))
        probs.append(expo * (1.0 / jnp.sum(expo, axis=1, keepdims=True)))
    return probs


def attn_fwd_kernel(scale, q_ref, kv_ref, kvo_ref, cos_ref, sin_ref, mask_ref, ctx_ref, qb_ref):
    mask = mask_ref[...] > 0.0
    for group in range(4):
        key2, val2 = kv_pair(kv_ref, kvo_ref, group)
        raw = stack_slabs(q_ref, group)
        query = (raw * cos_ref[...] + partner_half(raw) * sin_ref[...]).astype(jnp.bfloat16)
        write_slabs(qb_ref, group, query)
        probs = softmax_pair(query, key2, mask, scale)
        prob = jnp.concatenate([part.astype(jnp.bfloat16) for part in probs], axis=1)
        write_slabs(ctx_ref, group, kdot(prob, val2, 1, 0))


def attn_bwd_kernel(scale, qb_ref, dc_ref, kv_ref, kvo_ref, cos_ref, sin_ref, mask_ref, dq_ref, own_ref, oth_ref):
    mask = mask_ref[...] > 0.0
    keys = 2 * kv_ref.shape[0]
    local = kv_ref.shape[0]
    low = lane_of(keys) < HALF_SLAB
    held = {}
    for group in range(4):
        key2, val2 = kv_pair(kv_ref, kvo_ref, group)
        query = stack_slabs(qb_ref, group)
        d_ctx = stack_slabs(dc_ref, group)
        probs = softmax_pair(query, key2, mask, scale)
        d_prob = kdot(d_ctx, val2, 1, 1)
        d_scores = []
        for j in range(2):
            part = d_prob[:, j * LANES:(j + 1) * LANES]
            inner = jnp.sum(probs[j] * part, axis=1, keepdims=True)
            d_scores.append((probs[j] * (part - inner) * scale).astype(jnp.bfloat16))
        d_score = jnp.concatenate(d_scores, axis=1)
        prob = jnp.concatenate([part.astype(jnp.bfloat16) for part in probs], axis=1)
        d_query = kdot(d_score, key2, 1, 0)
        write_slabs(dq_ref, group, d_query * cos_ref[...] - partner_half(d_query) * sin_ref[...])
        for which, (lhs, rhs) in enumerate(((d_score, query), (prob, d_ctx))):
            both = kdot(lhs, rhs, 0, 0)
            top, bottom = both[:keys], both[keys:]
            if group % 2 == 0:
                held[which] = top + pltpu.roll(bottom, HALF_SLAB, 1)
            else:
                slab = jnp.where(low, held[which], bottom + pltpu.roll(top, HALF_SLAB, 1))
                at = (2 * which + group // 2) * LANES
                own_ref[:, at:at + LANES] = slab[:local]
                oth_ref[:, at:at + LANES] = slab[local:]


def cost(flops, nbytes):
    return pl.CostEstimate(flops=int(flops), bytes_accessed=int(nbytes), transcendentals=0)


VMEM_LIMIT = 48 * 1024 * 1024


def params():
    return pltpu.CompilerParams(dimension_semantics=("arbitrary",), vmem_limit_bytes=VMEM_LIMIT)


def norm_fwd(hidden, gain):
    hid32 = hidden.astype(jnp.float32)
    inv_rms = lax.rsqrt(jnp.mean(hid32 * hid32, axis=-1, keepdims=True) + NORM_EPS)
    return (hid32 * inv_rms * gain).astype(jnp.bfloat16), inv_rms


def norm_bwd(d_normed, hidden, inv_rms, gain):
    unit = hidden.astype(jnp.float32) * inv_rms
    d_unit = d_normed * gain
    d_hidden = inv_rms * (d_unit - unit * jnp.mean(d_unit * unit, axis=-1, keepdims=True))
    return d_hidden, jnp.sum(d_normed * unit, axis=0)


def gather_weight(shard):
    return lax.all_gather(shard, SHARD_AXES, axis=0, tiled=True)


def scatter_grad(local_grad):
    return lax.psum_scatter(local_grad, SHARD_AXES, scatter_dimension=0, tiled=True)


def solution(mesh):
    n_dev = mesh.shape["fsdp"] * mesh.shape["cp"]
    act_spec = P("fsdp", "cp", None)
    vec_spec = P(SHARD_AXES)
    mat_spec = P(SHARD_AXES, None)
    cube_spec = P(SHARD_AXES, None, None)
    bf16, f32 = jnp.bfloat16, jnp.float32

    def body(act_in, grad_out, positions, attn_norm, w_q, w_k, w_v, w_o, ffn_norm, w_gate, w_up, w_down):
        batch, seq, width = act_in.shape
        heads, head_dim = w_q.shape[1], w_q.shape[2]
        kv_heads = w_k.shape[1]
        rows = w_q.shape[0]
        q_cols, kv_cols = heads * head_dim, kv_heads * head_dim
        tokens = batch * seq
        scale = head_dim ** -0.5
        x = act_in.reshape(tokens, width)
        dy = grad_out.reshape(tokens, width)

        pos_f = jnp.concatenate([positions.astype(f32), jnp.zeros((rows - seq,), f32)])
        small = jnp.stack([attn_norm.astype(f32), ffn_norm.astype(f32), pos_f])
        small = lax.all_gather(small, SHARD_AXES, axis=0)
        gain1 = small[:, 0].reshape(-1)
        gain2 = small[:, 1].reshape(-1)
        pos_own = positions.astype(f32)
        pos_oth = jnp.where(lax.axis_index("cp") == 0, small[1, 2, :seq], small[0, 2, :seq])

        full_qkv = gather_weight(jnp.concatenate(
            [w_q.reshape(rows, q_cols), w_k.reshape(rows, kv_cols), w_v.reshape(rows, kv_cols)], axis=1))
        full_o = gather_weight(w_o)
        full_gate = gather_weight(w_gate)
        full_up = gather_weight(w_up)
        full_down = gather_weight(w_down)

        half = head_dim // 2
        inv_freq = jnp.power(ROPE_THETA, -(jnp.arange(half, dtype=f32) * (2.0 / head_dim)))
        angle = pos_own[:, None] * inv_freq[None, :]
        cos_t, sin_t = jnp.cos(angle), jnp.sin(angle)
        cos_t = jnp.concatenate([cos_t] * 4, axis=1)
        sin_t = jnp.concatenate([-sin_t, sin_t, -sin_t, sin_t], axis=1)
        cos_4, sin_4 = jnp.concatenate([cos_t] * 4, axis=0), jnp.concatenate([sin_t] * 4, axis=0)
        pos_keys = jnp.concatenate([pos_own, pos_oth])
        mask = (pos_keys[None, :] <= pos_own[:, None]).astype(f32)
        mask_4 = jnp.concatenate([mask] * 4, axis=0)

        whole = lambda arr: pl.BlockSpec(arr.shape, lambda b: (0, 0))
        q_blk = pl.BlockSpec((seq, q_cols), lambda b: (b, 0))
        kv_blk = pl.BlockSpec((seq, 2 * kv_cols), lambda b: (b, 0))
        t_blk = 4 * seq
        kv_in_blk = pl.BlockSpec((t_blk, 2 * kv_cols), lambda b: (b, q_cols // (2 * kv_cols)))
        kv_tall = pl.BlockSpec((t_blk, 2 * kv_cols), lambda b: (b, 0))
        pair_flops = 2 * tokens * heads * head_dim * 2 * seq

        normed, rms1 = norm_fwd(x, gain1)
        qkv = matmul("td,dn->tn", normed, full_qkv)
        kv = pl.pallas_call(
            rope_kv_kernel, grid=(tokens // t_blk,),
            in_specs=[kv_in_blk, whole(cos_t), whole(sin_t)], out_specs=kv_tall,
            out_shape=jax.ShapeDtypeStruct((tokens, 2 * kv_cols), bf16),
            compiler_params=params(), cost_estimate=cost(1e9, 6e6), name="rope_kv",
        )(qkv, cos_t, sin_t)
        swap = [(0, 1), (1, 0)]
        kv_oth = lax.ppermute(kv, "cp", swap)
        ctx, query = pl.pallas_call(
            functools.partial(attn_fwd_kernel, scale), grid=(batch,),
            in_specs=[q_blk, kv_blk, kv_blk, whole(cos_4), whole(sin_4), whole(mask_4)],
            out_specs=[q_blk, q_blk],
            out_shape=[jax.ShapeDtypeStruct((tokens, q_cols), bf16)] * 2,
            compiler_params=params(), cost_estimate=cost(4 * pair_flops, 40e6), name="attn_fwd",
        )(qkv, kv, kv_oth, cos_4, sin_4, mask_4)
        resid = (x.astype(f32) + matmul("tn,nd->td", ctx, full_o)).astype(bf16)
        normed2, rms2 = norm_fwd(resid, gain2)
        gate_pre = matmul("td,df->tf", normed2, full_gate)
        up_pre = matmul("td,df->tf", normed2, full_up)
        gate_sig = jax.nn.sigmoid(gate_pre)
        gate_act = gate_pre * gate_sig
        hidden = (gate_act * up_pre).astype(bf16)

        grad_down = matmul("tf,td->fd", hidden, dy)
        grad_down, dy, hidden = lax.optimization_barrier((grad_down, dy, hidden))
        grad_down = scatter_grad(grad_down) / n_dev
        d_hidden = matmul("td,fd->tf", dy, full_down)
        d_gate = (d_hidden * up_pre * gate_sig * (1.0 + gate_pre * (1.0 - gate_sig))).astype(bf16)
        d_up = (d_hidden * gate_act).astype(bf16)
        grad_gate = matmul("td,tf->df", normed2, d_gate)
        grad_gate, d_up = lax.optimization_barrier((grad_gate, d_up))
        grad_gate = scatter_grad(grad_gate) / n_dev
        grad_up = matmul("td,tf->df", normed2, d_up)
        grad_up, d_gate, d_up, hidden = lax.optimization_barrier((grad_up, d_gate, d_up, hidden))
        grad_up = scatter_grad(grad_up) / n_dev
        d_normed2 = matmul("tf,df->td", d_gate, full_gate)
        d_normed2 = d_normed2 + matmul("tf,df->td", d_up, full_up)
        d_resid, grad_ffn = norm_bwd(d_normed2, resid, rms2, gain2)
        d_resid = d_resid + dy.astype(f32)
        d_resid_half = d_resid.astype(bf16)
        grad_o = matmul("tn,td->nd", ctx, d_resid_half)
        grad_o, d_resid_half = lax.optimization_barrier((grad_o, d_resid_half))
        grad_o = scatter_grad(grad_o) / n_dev
        d_ctx = matmul("td,nd->tn", d_resid_half, full_o).astype(bf16)
        dq_wide, dkv_own, dkv_oth = pl.pallas_call(
            functools.partial(attn_bwd_kernel, scale), grid=(batch,),
            in_specs=[q_blk, q_blk, kv_blk, kv_blk, whole(cos_4), whole(sin_4), whole(mask_4)],
            out_specs=[q_blk, kv_blk, kv_blk],
            out_shape=[jax.ShapeDtypeStruct((tokens, q_cols + 2 * kv_cols), bf16)]
            + [jax.ShapeDtypeStruct((tokens, 2 * kv_cols), f32)] * 2,
            compiler_params=params(), cost_estimate=cost(10 * pair_flops, 50e6), name="attn_bwd",
        )(query, d_ctx, kv, kv_oth, cos_4, sin_4, mask_4)
        dkv_got = lax.ppermute(dkv_oth, "cp", swap)
        act_out = (resid.astype(f32) + matmul("tf,fd->td", hidden, full_down)).astype(bf16)
        d_qkv = pl.pallas_call(
            unrope_kv_kernel, grid=(tokens // t_blk,),
            in_specs=[kv_tall, kv_tall, whole(cos_t), whole(sin_t), pl.BlockSpec(memory_space=pl.ANY)],
            out_specs=kv_in_blk,
            out_shape=jax.ShapeDtypeStruct(dq_wide.shape, bf16),
            input_output_aliases={4: 0},
            compiler_params=params(), cost_estimate=cost(1e9, 10e6), name="unrope_kv",
        )(dkv_own, dkv_got, cos_t, sin_t, dq_wide)
        grad_qkv = matmul("td,tn->dn", normed, d_qkv)
        grad_qkv, d_qkv = lax.optimization_barrier((grad_qkv, d_qkv))
        grad_qkv = scatter_grad(grad_qkv) / n_dev
        d_normed = matmul("tn,dn->td", d_qkv, full_qkv)
        d_input, grad_attn = norm_bwd(d_normed, x, rms1, gain1)
        grad_in = (d_resid + d_input).astype(bf16)
        gains = jnp.stack([grad_attn.reshape(n_dev, rows), grad_ffn.reshape(n_dev, rows)], axis=1)
        gains = lax.psum_scatter(gains, SHARD_AXES, scatter_dimension=0, tiled=True)[0] / n_dev
        grad_q = grad_qkv[:, :q_cols].reshape(w_q.shape)
        grad_k = grad_qkv[:, q_cols:q_cols + kv_cols].reshape(w_k.shape)
        grad_v = grad_qkv[:, q_cols + kv_cols:].reshape(w_v.shape)
        shape = act_in.shape
        return (act_out.reshape(shape), grad_in.reshape(shape), gains[0], grad_q, grad_k, grad_v, grad_o, gains[1],
                grad_gate, grad_up, grad_down)

    in_specs = (act_spec, act_spec, P("cp"), vec_spec, cube_spec, cube_spec, cube_spec, mat_spec, vec_spec, mat_spec, mat_spec, mat_spec)
    out_specs = (act_spec, act_spec, vec_spec, cube_spec, cube_spec, cube_spec, mat_spec, vec_spec, mat_spec, mat_spec, mat_spec)
    return jax.shard_map(body, mesh=mesh, in_specs=in_specs, out_specs=out_specs, check_vma=False)
```

time: 3110 us -> 2050 us (0.66)
  matrix products: 1700 us -> 738 us
  local copies, waits for them, and re-layouts: 168 us -> 16.1 us
  Pallas kernels: 0 us -> 151 us
  other arithmetic: 140 us -> 83.6 us
  blocking collectives: 74 us -> 37.1 us
    dot_general x26 -> x15, matrix products: 1660 us -> 738 us  [matmul(): return jnp.einsum(form, lhs, rhs, preferred_element_type=jnp.float32)]
    all_gather x14 -> x5, waiting for transfers between devices: 323 us -> 89.7 us  [gather_weight(): return lax.all_gather(shard, SHARD_AXES, axis=0, tiled=True)]
    ppermute x0 -> x2, waiting for transfers between devices: none -> 170 us  [the longest x1 92.6 us: body(): dkv_got = lax.ppermute(dkv_oth, 'cp', swap)]
    pallas_call x0 -> x4, Pallas kernels: none -> 151 us  [the longest x1 88.8 us: body(): pl.pallas_call(functools.partial(attn_bwd_kernel, scale), grid=(batch,),...]
    unnamed x85 -> x61, local copies, waits for them, and re-layouts: 111 us -> 8.89 us
    reduce_scatter x7 -> x5, waiting for transfers between devices: 651 us -> 737 us  [scatter_grad(): lax.psum_scatter(local_grad, SHARD_AXES, scatter_dimension=0, tiled=True)]
    another operation x4 -> x3, other arithmetic: 69.4 us -> 1.33 us  [the longest x2 1.31 us: body(): small = jnp.stack([attn_norm.astype(f32), ffn_norm.astype(f32), pos_f])]
    all_gather x4 -> x1, blocking collectives: 46.5 us -> 13.4 us  [body(): small = lax.all_gather(small, SHARD_AXES, axis=0)]
  transfers between devices with their start and end apart: 25 -> 12, of which waited for: 12 -> 8; matrix products, arithmetic and copies ran while one was open for 47% -> 22% of each run, Pallas kernels for 0% -> 7%
where the time goes in v1:
time: 2050 us; the launch traced here: 2040 us
  waiting for transfers between devices  1000 us (49%)
  matrix products  738 us (36%)
  Pallas kernels  151 us (7%)
  other arithmetic  83.6 us (4%)
  blocking collectives  37.1 us (2%)
    dot_general x15, matrix products, matmul(): return jnp.einsum(form, lhs, rhs, preferred_element_type=jnp.float32)  738 us
    reduce_scatter x5, waiting for transfers between devices, scatter_grad(): lax.psum_scatter(local_grad, SHARD_AXES, scatter_dimension=0, tiled=True)  737 us
    ppermute x1, waiting for transfers between devices, body(): dkv_got = lax.ppermute(dkv_oth, 'cp', swap)  92.6 us
    all_gather x5, waiting for transfers between devices, gather_weight(): return lax.all_gather(shard, SHARD_AXES, axis=0, tiled=True)  89.7 us
    pallas_call x1, Pallas kernels, body(): pl.pallas_call(functools.partial(attn_bwd_kernel, scale), grid=(batch,),...  88.8 us
    ppermute x1, waiting for transfers between devices, body(): kv_oth = lax.ppermute(kv, 'cp', swap)  77.8 us
    pallas_call x1, Pallas kernels, body(): pl.pallas_call(functools.partial(attn_fwd_kernel, scale), grid=(batch,),...  49.4 us
  transfers between devices with their start and end apart: 12, of which 8 were waited for; matrix products, arithmetic and copies ran while one was open for 22% of the time, Pallas kernels for 7%

profile of v1, /device:TPU:0, one launch (start us, length us, event | category | flops | bytes accessed | tf_op | source)
XLA Modules:
  0.0 2042.4 jit_solution(4899495000142828508)
XLA Ops:
  20.1 13.4 all-gather.1
  33.7 8.8 fusion.17
  42.6 30.3 %all-gather.8.cloned.1.call-done = bf16[2048,2560]{0,1:T(8,128)(2,1)} async-done(((bf16[256,2560]{0,1:T(8,128)(2,1)}), bf16[2048,2560]{0,1:T(8,128)(2,1)}) %all-gather.8.cloned.1.call-update) | async-done | bytes 10485776 | tf_op jit(solution)/shard_map/all_gather | solution.py:171
  72.9 29.2 %fusion.40.kv_ref.q_ref = f32[2048,2560]{1,0:T(8,128)} fusion(bf16[2048,2048]{1,0:T(8,128)(2,1)} %fusion.17, bf16[2048,2560]{0,1:T(8,128)(2,1)} %all-gather.8.cloned.1.call-done), kind=kOutput, calls=%fused_computation.72 | convolution fusion | flops 21474836480 | bytes 39845888 | tf_op jit(solution)/shard_map/td,dn->tn/dot_general | solution.py:20
  108.6 77.8 %collective-permute-done.kvo_ref = bf16[2048,512]{1,0:T(8,128)(2,1)} collective-permute-done((bf16[2048,512]{1,0:T(8,128)(2,1)S(1)}, bf16[2048,512]{1,0:T(8,128)(2,1)}, u32[]{:S(2)}, u32[]{:S(2)}) %collective-permute-start) | collective-permute-done | bytes 2097184 | tf_op jit(solution)/shard_map/ppermute | solution.py:240
  186.4 49.4 %attn_fwd.1 = (bf16[2048,2048]{1,0:T(8,128)(2,1)}, bf16[2048,2048]{1,0:T(8,128)(2,1)}) custom-call(f32[2048,2560]{1,0:T(8,128)} %fusion.40.kv_ref.q_ref, bf16[2048,512]{1,0:T(8,128)(2,1)S(1)} %rope_kv.1.kv_ref, bf16[2048,512]{1,0:T(8,128)(2,1)} %collective-permute-done.kvo_ref, f32[256,128]{1,0:T(8,128)S(1)} %maximum_maximum_fusion.cos_ref, ...), custom_call_target="tpu_custom_call" | custom-call | flops 4294967296 | bytes 40000000 | tf_op jit(solution)/shard_map/attn_fwd/pallas_call | solution.py:241
  236.5 24.6 %fusion.11 = (f32[2048]{0:T(1024)S(1)}, bf16[2048,2048]{1,0:T(8,128)(2,1)}) fusion(bf16[2048,2048]{1,0:T(8,128)(2,1)} %get-tuple-element.29, bf16[2048,2048]{1,0:T(8,128)(2,1)} %all-gather.10.cloned.1.call-done, bf16[32,64,2048]{2,1,0:T(8,128)(2,1)} %param.12), kind=kOutput, calls=%fused_computation.18 | convolution fusion | flops 17205032960 | bytes 33562624 | tf_op jit(solution)/shard_map/tn,nd->td/dot_general | solution.py:20
  261.2 5.7 all-gather.12.cloned.1.call-done
  266.9 58.8 %fusion.35 = f32[2048,5632]{1,0:T(8,128)} fusion(bf16[2048,5632]{1,0:T(8,128)(2,1)} %all-gather.12.cloned.1.call-done, bf16[2048,2048]{1,0:T(8,128)(2,1)} %get-tuple-element.74, f32[2048]{0:T(1024)S(1)} %bitcast.95, f32[2048]{0:T(1024)S(1)} %add_rsqrt_fusion.1), kind=kOutput, calls=%fused_computation.68 | convolution fusion | flops 47261417472 | bytes 77611008 | tf_op jit(solution)/shard_map/td,df->tf/dot_general | solution.py:20
  325.6 53.7 %all-gather.14.cloned.1.call-done = bf16[2048,5632]{1,0:T(8,128)(2,1)} async-done(((bf16[256,5632]{1,0:T(8,128)(2,1)}), bf16[2048,5632]{1,0:T(8,128)(2,1)}) %all-gather.14.cloned.1.call-update) | async-done | bytes 23068688 | tf_op jit(solution)/shard_map/all_gather | solution.py:171
  379.3 67.3 %multiply_convert_fusion.2 = (bf16[2048,5632]{1,0:T(8,128)(2,1)}, f32[2048,5632]{1,0:T(8,128)}) fusion(f32[2048,5632]{1,0:T(8,128)} %fusion.35, bf16[2048,5632]{1,0:T(8,128)(2,1)} %all-gather.14.cloned.1.call-done, bf16[2048,2048]{1,0:T(8,128)(2,1)} %get-tuple-element.74, f32[2048]{0:T(1024)S(1)} %bitcast.96, f32[2048]{0:T(1024)S(1)} %add_rsqrt_fusion.1), kind=kOutput, calls=%fused_computation.2 | convolution fusion | flops 47330623488 | bytes 146817024 | tf_op jit(solution)/shard_map/td,df->tf/dot_general | solution.py:20
  446.6 58.6 %fusion.41 = f32[5632,2048]{1,0:T(8,128)} fusion(bf16[2048,5632]{1,0:T(8,128)(2,1)} %get-tuple-element.33, bf16[2048,2048]{1,0:T(8,128)(2,1)} %bitcast.79), kind=kOutput, calls=%fused_computation.73 | convolution fusion | flops 47244640256 | bytes 77594624 | tf_op jit(solution)/shard_map/tf,td->fd/dot_general | solution.py:20
  505.2 85.1 %multiply_convert_fusion = (bf16[2048,5632]{1,0:T(8,128)(2,1)}, bf16[2048,5632]{1,0:T(8,128)(2,1)}) fusion(f32[2048,5632]{1,0:T(8,128)} %fusion.35, f32[2048,5632]{1,0:T(8,128)} %get-tuple-element.76, bf16[2048,2048]{1,0:T(8,128)(2,1)} %bitcast.80, bf16[5632,2048]{1,0:T(8,128)(2,1)} %all-gather.16.cloned.1.call-done), kind=kOutput, calls=%fused_computation | convolution fusion | flops 47394586624 | bytes 169869312 | tf_op jit(solution)/shard_map/td,fd->tf/dot_general | solution.py:20
  590.3 60.2 %fusion.31 = f32[2048,5632]{1,0:T(8,128)} fusion(bf16[2048,5632]{1,0:T(8,128)(2,1)} %get-tuple-element.34, bf16[2048,2048]{1,0:T(8,128)(2,1)} %get-tuple-element.74, f32[2048]{0:T(1024)S(1)} %bitcast.97, f32[2048]{0:T(1024)S(1)} %copy-done.18), kind=kOutput, calls=%fused_computation.66 | convolution fusion | flops 47261417472 | bytes 77611008 | tf_op jit(solution)/shard_map/td,tf->df/dot_general | solution.py:20
  650.5 60.4 %fusion.29 = f32[2048,5632]{1,0:T(8,128)} fusion(bf16[2048,5632]{1,0:T(8,128)(2,1)} %get-tuple-element.35, bf16[2048,2048]{1,0:T(8,128)(2,1)} %get-tuple-element.74, f32[2048]{0:T(1024)S(1)} %bitcast.98, f32[2048]{0:T(1024)S(1)} %copy-done.18), kind=kOutput, calls=%fused_computation.65 | convolution fusion | flops 47261417472 | bytes 77611008 | tf_op jit(solution)/shard_map/td,tf->df/dot_general | solution.py:20
  710.8 60.1 %fusion.42 = f32[2048,2048]{1,0:T(8,128)} fusion(bf16[2048,5632]{1,0:T(8,128)(2,1)} %get-tuple-element.34, bf16[2048,5632]{1,0:T(8,128)(2,1)} %all-gather.12.cloned.1.call-done), kind=kOutput, calls=%fused_computation.74 | convolution fusion | flops 47244640256 | bytes 62914560 | tf_op jit(solution)/shard_map/tf,df->td/dot_general | solution.py:20
  771.0 68.5 %fusion.10 = (f32[2048]{0:T(1024)}, f32[2048]{0:T(1024)S(1)}, f32[2048,2048]{1,0:T(8,128)}) fusion(bf16[2048,2048]{1,0:T(8,128)(2,1)} %get-tuple-element.74, f32[2048]{0:T(1024)S(1)} %copy-done.18, f32[2048]{0:T(1024)S(1)} %bitcast.99, f32[2048,2048]{1,0:T(8,128)} %fusion.42, bf16[2048,5632]{1,0:T(8,128)(2,1)} %get-tuple-element.35, ...), kind=kOutput, calls=%fused_computation.17 | convolution fusion | flops 47278194688 | bytes 88113152 | tf_op jit(solution)/shard_map/tf,df->td/dot_general | solution.py:20
  839.4 12.3 fusion.28
  855.1 21.2 %fusion.43 = f32[2048,2048]{1,0:T(8,128)} fusion(bf16[2048,2048]{1,0:T(8,128)(2,1)S(1)} %copy-done.26, bf16[2048,2048]{1,0:T(8,128)(2,1)S(1)} %fusion.28), kind=kOutput, calls=%fused_computation.75 | convolution fusion | flops 17179869184 | bytes 33554432 | tf_op jit(solution)/shard_map/tn,td->nd/dot_general | solution.py:20
  876.4 25.0 %convolution_convert_fusion.dc_ref = bf16[2048,2048]{1,0:T(8,128)(2,1)} fusion(bf16[2048,2048]{1,0:T(8,128)(2,1)} %copy-done.11, bf16[2048,2048]{1,0:T(8,128)(2,1)} %all-gather.10.cloned.1.call-done), kind=kOutput, calls=%fused_computation.37 | convolution fusion | flops 17184063488 | bytes 25165824 | tf_op jit(solution)/shard_map/td,nd->tn/dot_general | solution.py:20
  901.5 88.8 %attn_bwd.1 = (bf16[2048,2560]{1,0:T(8,128)(2,1)}, f32[2048,512]{1,0:T(8,128)}, f32[2048,512]{1,0:T(8,128)}) custom-call(bf16[2048,2048]{1,0:T(8,128)(2,1)} %get-tuple-element.36.qb_ref, bf16[2048,2048]{1,0:T(8,128)(2,1)} %convolution_convert_fusion.dc_ref, bf16[2048,512]{1,0:T(8,128)(2,1)S(1)} %rope_kv.1.kv_ref, ...), custom_call_target="tpu_custom_call" | custom-call | flops 10737418240 | bytes 50000000 | tf_op jit(solution)/shard_map/attn_bwd/pallas_call | solution.py:277
  990.3 92.6 %collective-permute-done.1.got_ref = f32[2048,512]{1,0:T(8,128)S(1)} collective-permute-done((f32[2048,512]{1,0:T(8,128)}, f32[2048,512]{1,0:T(8,128)S(1)}, u32[]{:S(2)}, u32[]{:S(2)}) %collective-permute-start.1) | collective-permute-done | bytes 4194336 | tf_op jit(solution)/shard_map/ppermute | solution.py:285
  1087.1 6.8 unrope_kv.1
  1093.9 26.5 %fusion.44 = f32[2048,2560]{1,0:T(8,128)} fusion(bf16[2048,2048]{1,0:T(8,128)(2,1)S(1)} %bitcast.85, bf16[2048,2560]{1,0:T(8,128)(2,1)} %unrope_kv.1), kind=kOutput, calls=%fused_computation.76 | convolution fusion | flops 21474836480 | bytes 39845888 | tf_op jit(solution)/shard_map/td,tn->dn/dot_general | solution.py:20
  1123.2 60.8 %fusion.12 = bf16[2048,2048]{1,0:T(8,128)(2,1)} fusion(bf16[2048,2048]{1,0:T(8,128)(2,1)} %get-tuple-element.74, bf16[2048,5632]{1,0:T(8,128)(2,1)} %get-tuple-element.33, bf16[5632,2048]{1,0:T(8,128)(2,1)} %all-gather.16.cloned.1.call-done), kind=kOutput, calls=%fused_computation.19 | convolution fusion | flops 47257223168 | bytes 62914560 | tf_op jit(solution)/shard_map/tf,fd->td/dot_general | solution.py:20
  1184.0 31.4 %fusion.23 = (f32[2048]{0:T(1024)S(1)}, f32[2048]{0:T(1024)S(1)}, f32[2048,2048]{1,0:T(8,128)}) fusion(bf16[32,64,2048]{2,1,0:T(8,128)(2,1)} %param.12, f32[2048]{0:T(1024)S(1)} %copy-done.14, f32[2048]{0:T(1024)S(1)} %bitcast.93, bf16[2048,2560]{1,0:T(8,128)(2,1)} %unrope_kv.1, bf16[2048,2560]{0,1:T(8,128)(2,1)} %all-gather.8.cloned.1.call-done), kind=kOutput, calls=%fused_computation.33 | convolution fusion | flops 21504192512 | bytes 46170112 | tf_op jit(solution)/shard_map/tn,dn->td/dot_general | solution.py:20
  1215.4 23.8 %all-reduce.1 = f32[8,2,256]{2,1,0:T(2,128)S(1)} all-reduce(f32[8,2,256]{2,1,0:T(2,128)S(1)} %pad_maximum_fusion.3), channel_id=3, replica_groups=mesh['cp'=2,'fsdp'=4] {'fsdp','cp'}, use_global_device_ids=true, to_apply=%region_6.7.clone | all-reduce | flops 4096 | bytes 32768
  1240.4 27.2 %fusion.22 = bf16[2048,2048]{1,0:T(8,128)(2,1)} fusion(bf16[32,64,2048]{2,1,0:T(8,128)(2,1)} %param.12, f32[2048,2048]{1,0:T(8,128)} %get-tuple-element.78, f32[2048]{0:T(1024)S(1)} %broadcast_multiply_fusion.5, f32[2048]{0:T(1024)S(1)} %bitcast.94, f32[2048]{0:T(1024)S(1)} %copy-done.14, bf16[2048,2048]{1,0:T(8,128)(2,1)} %bitcast.82, ...), kind=kLoop, calls=%fused_computation.32 | loop fusion | flops 67108864 | bytes 67158016 | tf_op jit(solution)/shard_map/convert_element_type | solution.py:300
  1280.6 229.2 %reduce-scatter.14.cloned.1.call-done = f32[704,2048]{1,0:T(8,128)} async-done(((f32[5632,2048]{1,0:T(8,128)}), f32[704,2048]{1,0:T(8,128)}) %reduce-scatter.14.cloned.1.call-update) | async-done | bytes 5767184 | tf_op jit(solution)/shard_map/reduce_scatter | solution.py:175
  1509.8 6.1 broadcast_multiply_fusion
  1516.0 253.9 %reduce-scatter.10.cloned.1.call-done = f32[256,5632]{1,0:T(8,128)} async-done(((f32[2048,5632]{1,0:T(8,128)}), f32[256,5632]{1,0:T(8,128)}) %reduce-scatter.10.cloned.1.call-update) | async-done | bytes 5767184 | tf_op jit(solution)/shard_map/reduce_scatter | solution.py:175
  1775.5 254.3 %reduce-scatter.12.cloned.1.call-done = f32[256,5632]{1,0:T(8,128)} async-done(((f32[2048,5632]{1,0:T(8,128)}), f32[256,5632]{1,0:T(8,128)}) %reduce-scatter.12.cloned.1.call-update) | async-done | bytes 5767184 | tf_op jit(solution)/shard_map/reduce_scatter | solution.py:175
  (123 shorter events, 55.8 us)
Async XLA Ops:
  7.2 65.7 %all-gather.8.cloned.1.call-start = ((), (), s32[]{:S(2)}) async-start(), calls=%async_computation.5 | async-start | bytes 11796480 | tf_op jit(solution)/shard_map/all_gather | solution.py:171
  9.8 226.7 %all-gather.10.cloned.1.call-start = ((), (), s32[]{:S(2)}) async-start(), calls=%async_computation.6 | async-start | bytes 9437184 | tf_op jit(solution)/shard_map/all_gather | solution.py:171
  10.5 256.3 %all-gather.12.cloned.1.call-start = ((), (), s32[]{:S(2)}) async-start(), calls=%async_computation.7 | async-start | bytes 25952256 | tf_op jit(solution)/shard_map/all_gather | solution.py:171
  11.2 368.1 %all-gather.14.cloned.1.call-start = ((), (), s32[]{:S(2)}) async-start(), calls=%async_computation.8 | async-start | bytes 25952256 | tf_op jit(solution)/shard_map/all_gather | solution.py:171
  11.8 493.4 %all-gather.16.cloned.1.call-start = ((), (), s32[]{:S(2)}) async-start(), calls=%async_computation.9 | async-start | bytes 25952256 | tf_op jit(solution)/shard_map/all_gather | solution.py:171
  12.4 1255.2 %reduce-scatter.8.cloned.1.call-start = ((), (), s32[]{:S(2)}) async-start(), calls=%async_computation.11 | async-start | bytes 18874368 | tf_op jit(solution)/shard_map/reduce_scatter | solution.py:175
  20.1 82.1 %copy-start.13 = (f32[2048]{0:T(1024)}, f32[2048]{0:T(1024)S(1)}, u32[]{:S(2)}) copy-start(f32[2048]{0:T(1024)S(1)} %rsqrt.20) | copy-start | bytes 24580
  33.5 345.8 %copy-start.22 = (f32[8,1,256]{2,1,0:T(1,128)}, f32[8,1,256]{2,1,0:T(1,128)S(1)}, u32[]{:S(2)}) copy-start(f32[8,1,256]{2,1,0:T(1,128)S(1)} %get-tuple-element.66) | copy-start | bytes 24580
  42.6 59.6 %copy-start.7 = (f32[64,128]{1,0:T(8,128)}, f32[64,128]{1,0:T(8,128)S(1)}, u32[]{:S(2)}) copy-start(f32[64,128]{1,0:T(8,128)S(1)} %get-tuple-element.79.cos_ref) | copy-start | bytes 98308
  42.6 59.5 %copy-start.9 = (f32[64,128]{1,0:T(8,128)}, f32[64,128]{1,0:T(8,128)S(1)}, u32[]{:S(2)}) copy-start(f32[64,128]{1,0:T(8,128)S(1)} %get-tuple-element.80.sin_ref) | copy-start | bytes 98308
  107.6 78.8 %collective-permute-start = (bf16[2048,512]{1,0:T(8,128)(2,1)S(1)}, bf16[2048,512]{1,0:T(8,128)(2,1)}, u32[]{:S(2)}, u32[]{:S(2)}) collective-permute-start(bf16[2048,512]{1,0:T(8,128)(2,1)S(1)} %rope_kv.1.kv_ref), channel_id=1, source_target_pairs={{0,4},{4,0},{1,5},{5,1},{2,6},{6,2},{3,7},{7,3}} | collective-permute-start | bytes 6291464 | tf_op jit(solution)/shard_map/ppermute | solution.py:240
  108.3 78.1 %copy-start.3 = (f32[256,128]{1,0:T(8,128)}, f32[256,128]{1,0:T(8,128)S(1)}, u32[]{:S(2)}) copy-start(f32[256,128]{1,0:T(8,128)S(1)} %maximum_maximum_fusion.1.sin_ref) | copy-start | bytes 393220
  108.5 77.9 %copy-start.1 = (f32[256,128]{1,0:T(8,128)}, f32[256,128]{1,0:T(8,128)S(1)}, u32[]{:S(2)}) copy-start(f32[256,128]{1,0:T(8,128)S(1)} %maximum_maximum_fusion.cos_ref) | copy-start | bytes 393220
  261.1 118.2 %copy-start.17 = (f32[2048]{0:T(1024)}, f32[2048]{0:T(1024)S(1)}, u32[]{:S(2)}) copy-start(f32[2048]{0:T(1024)S(1)} %add_rsqrt_fusion.1) | copy-start | bytes 24580
  505.2 85.1 %copy-start.18 = (f32[2048]{0:T(1024)S(1)}, f32[2048]{0:T(1024)}, u32[]{:S(2)}) copy-start(f32[2048]{0:T(1024)} %copy-done.17) | copy-start | bytes 24580
  505.2 85.1 %copy-start.23 = (f32[8,1,256]{2,1,0:T(1,128)S(1)}, f32[8,1,256]{2,1,0:T(1,128)}, u32[]{:S(2)}) copy-start(f32[8,1,256]{2,1,0:T(1,128)} %copy-done.22) | copy-start | bytes 24580
  876.3 25.1 %copy-start.2 = (f32[256,128]{1,0:T(8,128)S(1)}, f32[256,128]{1,0:T(8,128)}, u32[]{:S(2)}) copy-start(f32[256,128]{1,0:T(8,128)} %copy-done.1) | copy-start | bytes 393220
  876.3 395.1 %reduce-scatter.6.cloned.1.call-start = ((), (), s32[]{:S(2)}) async-start(), calls=%async_computation.10 | async-start | bytes 23592960 | tf_op jit(solution)/shard_map/reduce_scatter | solution.py:175
  901.4 192.5 %slice-start = ((s8[8388608]{0:T(1024)(128)(4,1)}), s8[4194304]{0:T(1024)(128)(4,1)S(1)}, s32[]{:S(2)}) async-start(s8[8388608]{0:T(1024)(128)(4,1)} %bitcast.84), calls=%async_computation.15 | async-start | bytes 8388608
  901.4 183.4 %copy-start.8 = (f32[64,128]{1,0:T(8,128)S(1)}, f32[64,128]{1,0:T(8,128)}, u32[]{:S(2)}) copy-start(f32[64,128]{1,0:T(8,128)} %copy-done.7) | copy-start | bytes 98308
  901.5 183.4 %copy-start.10 = (f32[64,128]{1,0:T(8,128)S(1)}, f32[64,128]{1,0:T(8,128)}, u32[]{:S(2)}) copy-start(f32[64,128]{1,0:T(8,128)} %copy-done.9) | copy-start | bytes 98308
  901.5 192.5 %slice-start.1 = ((s8[8388608]{0:T(1024)(128)(4,1)}), s8[4194304]{0:T(1024)(128)(4,1)S(1)}, s32[]{:S(2)}) async-start(s8[8388608]{0:T(1024)(128)(4,1)} %bitcast.84), calls=%async_computation.16 | async-start | bytes 8388608
  990.3 92.6 %collective-permute-start.1 = (f32[2048,512]{1,0:T(8,128)}, f32[2048,512]{1,0:T(8,128)S(1)}, u32[]{:S(2)}, u32[]{:S(2)}) collective-permute-start(f32[2048,512]{1,0:T(8,128)} %get-tuple-element.39), channel_id=1, source_target_pairs={{0,4},{4,0},{1,5},{5,1},{2,6},{6,2},{3,7},{7,3}} | collective-permute-start | bytes 12582920 | tf_op jit(solution)/shard_map/ppermute | solution.py:285
  1120.4 389.4 %reduce-scatter.14.cloned.1.call-start = ((), (), s32[]{:S(2)}) async-start(), calls=%async_computation.14 | async-start | bytes 51904512 | tf_op jit(solution)/shard_map/reduce_scatter | solution.py:175
  1121.2 648.7 %reduce-scatter.10.cloned.1.call-start = ((), (), s32[]{:S(2)}) async-start(), calls=%async_computation.12 | async-start | bytes 51904512 | tf_op jit(solution)/shard_map/reduce_scatter | solution.py:175
  1121.9 907.8 %reduce-scatter.12.cloned.1.call-start = ((), (), s32[]{:S(2)}) async-start(), calls=%async_computation.13 | async-start | bytes 51904512 | tf_op jit(solution)/shard_map/reduce_scatter | solution.py:175
  1123.2 60.8 %copy-start.14 = (f32[2048]{0:T(1024)S(1)}, f32[2048]{0:T(1024)}, u32[]{:S(2)}) copy-start(f32[2048]{0:T(1024)} %copy-done.13) | copy-start | bytes 24580
  1123.2 60.8 %copy-start.16 = (f32[8,1,256]{2,1,0:T(1,128)S(1)}, f32[8,1,256]{2,1,0:T(1,128)}, u32[]{:S(2)}) copy-start(f32[8,1,256]{2,1,0:T(1,128)} %copy-done.15) | copy-start | bytes 24580
  1183.9 31.5 %copy-start.25 = (f32[2048]{0:T(1024)S(1)}, f32[2048]{0:T(1024)}, u32[]{:S(2)}) copy-start(f32[2048]{0:T(1024)} %get-tuple-element.60) | copy-start | bytes 24580
  1183.9 56.5 %copy-start.19 = (f32[2048]{0:T(1024)S(1)}, f32[2048]{0:T(1024)}, u32[]{:S(2)}) copy-start(f32[2048]{0:T(1024)} %copy-done.17) | copy-start | bytes 24580
  1183.9 56.5 %copy-start.21 = (f32[2048]{0:T(1024)S(1)}, f32[2048]{0:T(1024)}, u32[]{:S(2)}) copy-start(f32[2048]{0:T(1024)} %copy-done.20) | copy-start | bytes 24580
  1184.0 56.5 %copy-start.24 = (f32[8,1,256]{2,1,0:T(1,128)S(1)}, f32[8,1,256]{2,1,0:T(1,128)}, u32[]{:S(2)}) copy-start(f32[8,1,256]{2,1,0:T(1,128)} %copy-done.22) | copy-start | bytes 24580
  (10 other events, 96.0 us)
Sparse Core Ops, SparseCore 0:
  10.4 62.4 all-gather.7
  74.7 59.7 all-gather.9
  136.3 130.4 all-gather.11
  268.5 110.7 all-gather.13
  381.0 110.7 all-gather.15
  876.4 107.4 reduce-scatter.7
  1120.6 129.1 reduce-scatter.5
  1253.3 256.4 reduce-scatter.13
  1513.4 256.4 reduce-scatter.9
  1773.3 256.4 reduce-scatter.11

commit v2 on v1

--- a/solution.py
+++ b/solution.py
@@ -175,6 +175,42 @@
     return lax.psum_scatter(local_grad, SHARD_AXES, scatter_dimension=0, tiled=True)
 
 
+SWAP_CORE = ("fsdp", [(0, 1), (1, 0), (2, 3), (3, 2)])
+SWAP_X = ("fsdp", [(0, 2), (2, 0), (1, 3), (3, 1)])
+SWAP_Y = ("cp", [(0, 1), (1, 0)])
+
+
+def swap(vals, how):
+    return lax.ppermute(vals, how[0], how[1])
+
+
+def relative_blocks(lhs, order):
+    block = lhs.shape[1] // 8
+    place = lax.axis_index("fsdp")
+    x_at, core, y_at = place // 2, place % 2, lax.axis_index("cp")
+    sides = []
+    for d_core in (0, 1):
+        halves = []
+        for first in (0, 1):
+            for second in (0, 1):
+                d_x, d_y = (first, second) if order == "x" else (second, first)
+                owner = (((x_at + d_x) % 2) * 2 + (core + d_core) % 2) * 2 + (y_at + d_y) % 2
+                halves.append(lax.dynamic_slice_in_dim(lhs, owner * block, block, 1))
+        sides.append(halves)
+    return sides
+
+
+def partner_part(blocks, rhs, scale):
+    return matmul("td,tn->dn", jnp.concatenate(blocks[1], axis=1), rhs) * scale
+
+
+def own_parts(blocks, rhs, got, scale):
+    cut = got.shape[0] // 2
+    far = matmul("td,tn->dn", jnp.concatenate(blocks[0][2:], axis=1), rhs) * scale + got[cut:]
+    near = matmul("td,tn->dn", jnp.concatenate(blocks[0][:2], axis=1), rhs) * scale + got[:cut]
+    return far, near
+
+
 def solution(mesh):
     n_dev = mesh.shape["fsdp"] * mesh.shape["cp"]
     act_spec = P("fsdp", "cp", None)
@@ -191,6 +227,7 @@
         q_cols, kv_cols = heads * head_dim, kv_heads * head_dim
         tokens = batch * seq
         scale = head_dim ** -0.5
+        share = 1.0 / n_dev
         x = act_in.reshape(tokens, width)
         dy = grad_out.reshape(tokens, width)
 
@@ -236,8 +273,7 @@
             out_shape=jax.ShapeDtypeStruct((tokens, 2 * kv_cols), bf16),
             compiler_params=params(), cost_estimate=cost(1e9, 6e6), name="rope_kv",
         )(qkv, cos_t, sin_t)
-        swap = [(0, 1), (1, 0)]
-        kv_oth = lax.ppermute(kv, "cp", swap)
+        kv_oth = swap(kv, SWAP_Y)
         ctx, query = pl.pallas_call(
             functools.partial(attn_fwd_kernel, scale), grid=(batch,),
             in_specs=[q_blk, kv_blk, kv_blk, whole(cos_4), whole(sin_4), whole(mask_4)],
@@ -253,27 +289,35 @@
         gate_act = gate_pre * gate_sig
         hidden = (gate_act * up_pre).astype(bf16)
 
-        grad_down = matmul("tf,td->fd", hidden, dy)
+        grad_down = matmul("tf,td->fd", hidden, dy) * share
         grad_down, dy, hidden = lax.optimization_barrier((grad_down, dy, hidden))
-        grad_down = scatter_grad(grad_down) / n_dev
+        grad_down = scatter_grad(grad_down)
         d_hidden = matmul("td,fd->tf", dy, full_down)
         d_gate = (d_hidden * up_pre * gate_sig * (1.0 + gate_pre * (1.0 - gate_sig))).astype(bf16)
         d_up = (d_hidden * gate_act).astype(bf16)
-        grad_gate = matmul("td,tf->df", normed2, d_gate)
-        grad_gate, d_up = lax.optimization_barrier((grad_gate, d_up))
-        grad_gate = scatter_grad(grad_gate) / n_dev
-        grad_up = matmul("td,tf->df", normed2, d_up)
-        grad_up, d_gate, d_up, hidden = lax.optimization_barrier((grad_up, d_gate, d_up, hidden))
-        grad_up = scatter_grad(grad_up) / n_dev
+        blocks2 = relative_blocks(normed2, "y")
+        gate_oth = partner_part(blocks2, d_gate, share)
+        gate_oth, d_up = lax.optimization_barrier((gate_oth, d_up))
+        gate_got = swap(gate_oth, SWAP_CORE)
+        grad_up = matmul("td,tf->df", normed2, d_up) * share
+        grad_up, d_gate, hidden = lax.optimization_barrier((grad_up, d_gate, hidden))
+        grad_up = scatter_grad(grad_up)
+        gate_far, gate_near = own_parts(blocks2, d_gate, gate_got, share)
+        gate_far, gate_near, d_gate, d_up = lax.optimization_barrier((gate_far, gate_near, d_gate, d_up))
+        gate_got = swap(gate_far, SWAP_Y)
         d_normed2 = matmul("tf,df->td", d_gate, full_gate)
         d_normed2 = d_normed2 + matmul("tf,df->td", d_up, full_up)
         d_resid, grad_ffn = norm_bwd(d_normed2, resid, rms2, gain2)
         d_resid = d_resid + dy.astype(f32)
         d_resid_half = d_resid.astype(bf16)
-        grad_o = matmul("tn,td->nd", ctx, d_resid_half)
-        grad_o, d_resid_half = lax.optimization_barrier((grad_o, d_resid_half))
-        grad_o = scatter_grad(grad_o) / n_dev
+        blocks_o = relative_blocks(ctx, "y")
+        o_oth = partner_part(blocks_o, d_resid_half, share)
+        o_oth, d_resid_half = lax.optimization_barrier((o_oth, d_resid_half))
+        o_got = swap(o_oth, SWAP_CORE)
         d_ctx = matmul("td,nd->tn", d_resid_half, full_o).astype(bf16)
+        d_ctx, d_resid_half = lax.optimization_barrier((d_ctx, d_resid_half))
+        o_far, o_near = own_parts(blocks_o, d_resid_half, o_got, share)
+        o_far, o_near, d_ctx = lax.optimization_barrier((o_far, o_near, d_ctx))
         dq_wide, dkv_own, dkv_oth = pl.pallas_call(
             functools.partial(attn_bwd_kernel, scale), grid=(batch,),
             in_specs=[q_blk, q_blk, kv_blk, kv_blk, whole(cos_4), whole(sin_4), whole(mask_4)],
@@ -282,8 +326,24 @@
             + [jax.ShapeDtypeStruct((tokens, 2 * kv_cols), f32)] * 2,
             compiler_params=params(), cost_estimate=cost(10 * pair_flops, 50e6), name="attn_bwd",
         )(query, d_ctx, kv, kv_oth, cos_4, sin_4, mask_4)
-        dkv_got = lax.ppermute(dkv_oth, "cp", swap)
+        dkv_got = swap(dkv_oth, SWAP_Y)
+        o_got = swap(o_far, SWAP_Y)
+        cut = q_cols // 2
+        dq_parts = (dq_wide[:, :cut], dq_wide[:, cut:q_cols])
+        q_blocks = (relative_blocks(normed, "x"), relative_blocks(normed, "y"))
+        q_oth = [partner_part(blocks, part, share) for blocks, part in zip(q_blocks, dq_parts)]
+        q_oth[0], q_oth[1], hidden = lax.optimization_barrier((q_oth[0], q_oth[1], hidden))
+        q_got = [swap(part, SWAP_CORE) for part in q_oth]
         act_out = (resid.astype(f32) + matmul("tf,fd->td", hidden, full_down)).astype(bf16)
+        act_out, dq_parts = lax.optimization_barrier((act_out, dq_parts))
+        q_both = [own_parts(*args, share) for args in zip(q_blocks, dq_parts, q_got)]
+        q_both, gate_near = lax.optimization_barrier((q_both, gate_near))
+        q_got = [swap(q_both[0][0], SWAP_X), swap(q_both[1][0], SWAP_Y)]
+        cut = rows
+        gate_send = gate_near[cut:] + gate_got[cut:]
+        gate_last = swap(gate_send, SWAP_X)
+        o_send = o_near[cut:] + o_got[cut:]
+        o_last = swap(o_send, SWAP_X)
         d_qkv = pl.pallas_call(
             unrope_kv_kernel, grid=(tokens // t_blk,),
             in_specs=[kv_tall, kv_tall, whole(cos_t), whole(sin_t), pl.BlockSpec(memory_space=pl.ANY)],
@@ -292,17 +352,22 @@
             input_output_aliases={4: 0},
             compiler_params=params(), cost_estimate=cost(1e9, 10e6), name="unrope_kv",
         )(dkv_own, dkv_got, cos_t, sin_t, dq_wide)
-        grad_qkv = matmul("td,tn->dn", normed, d_qkv)
-        grad_qkv, d_qkv = lax.optimization_barrier((grad_qkv, d_qkv))
-        grad_qkv = scatter_grad(grad_qkv) / n_dev
+        grad_kv = matmul("td,tn->dn", normed, d_qkv[:, q_cols:]) * share
+        grad_kv, d_qkv = lax.optimization_barrier((grad_kv, d_qkv))
+        grad_kv = scatter_grad(grad_kv)
+        q_send = [both[1][cut:] + got[cut:] for both, got in zip(q_both, q_got)]
+        q_last = [swap(q_send[0], SWAP_Y), swap(q_send[1], SWAP_X)]
         d_normed = matmul("tn,dn->td", d_qkv, full_qkv)
         d_input, grad_attn = norm_bwd(d_normed, x, rms1, gain1)
         grad_in = (d_resid + d_input).astype(bf16)
         gains = jnp.stack([grad_attn.reshape(n_dev, rows), grad_ffn.reshape(n_dev, rows)], axis=1)
-        gains = lax.psum_scatter(gains, SHARD_AXES, scatter_dimension=0, tiled=True)[0] / n_dev
-        grad_q = grad_qkv[:, :q_cols].reshape(w_q.shape)
-        grad_k = grad_qkv[:, q_cols:q_cols + kv_cols].reshape(w_k.shape)
-        grad_v = grad_qkv[:, q_cols + kv_cols:].reshape(w_v.shape)
+        gains = lax.psum_scatter(gains, SHARD_AXES, scatter_dimension=0, tiled=True)[0] * share
+        grad_gate = gate_near[:cut] + gate_got[:cut] + gate_last
+        grad_o = o_near[:cut] + o_got[:cut] + o_last
+        grad_q = jnp.concatenate([both[1][:cut] + got[:cut] + last
+                                  for both, got, last in zip(q_both, q_got, q_last)], axis=1).reshape(w_q.shape)
+        grad_k = grad_kv[:, :kv_cols].reshape(w_k.shape)
+        grad_v = grad_kv[:, kv_cols:].reshape(w_v.shape)
         shape = act_in.shape
         return (act_out.reshape(shape), grad_in.reshape(shape), gains[0], grad_q, grad_k, grad_v, grad_o, gains[1],
                 grad_gate, grad_up, grad_down)

time: 2050 us -> 2010 us (0.980)
  waiting for transfers between devices: 1000 us -> 743 us
  blocking collectives: 37.1 us -> 178 us
  matrix products: 738 us -> 778 us
    reduce_scatter x5 -> x3, waiting for transfers between devices: 737 us -> 36.6 us  [scatter_grad(): lax.psum_scatter(local_grad, SHARD_AXES, scatter_dimension=0, tiled=True)]
    ppermute x2 -> x14, waiting for transfers between devices: 170 us -> 628 us  [swap(): return lax.ppermute(vals, how[0], how[1])]
    unnamed x1, blocking collectives: 23.8 us -> 165 us
    dot_general x15 -> x25, matrix products: 738 us -> 778 us  [matmul(): return jnp.einsum(form, lhs, rhs, preferred_element_type=jnp.float32)]
    add x0 -> x8, other arithmetic: none -> 29.7 us  [the longest x1 10.2 us: body(): grad_gate = gate_near[:cut] + gate_got[:cut] + gate_last]
    div x6 -> x0, other arithmetic: 24.3 us -> none  [the longest x1 6.15 us: body(): grad_down = scatter_grad(grad_down) / n_dev]
  transfers between devices with their start and end apart: 12 -> 22, of which waited for: 8 -> 9; matrix products, arithmetic and copies ran while one was open for 22% -> 28% of each run, Pallas kernels for 7% -> 3%
where the time goes in v2:
time: 2010 us; the launch traced here: 2000 us
  matrix products  778 us (39%)
  waiting for transfers between devices  743 us (37%)
  blocking collectives  178 us (9%)
  Pallas kernels  150 us (7%)
  other arithmetic  93 us (5%)
  local copies, waits for them, and re-layouts  32.3 us (2%)
    dot_general x25, matrix products, matmul(): return jnp.einsum(form, lhs, rhs, preferred_element_type=jnp.float32)  778 us
    ppermute x14, waiting for transfers between devices, swap(): return lax.ppermute(vals, how[0], how[1])  628 us
    unnamed x1, blocking collectives  165 us
    pallas_call x1, Pallas kernels, body(): pl.pallas_call(functools.partial(attn_bwd_kernel, scale), grid=(batch,),...  88.7 us
    all_gather x5, waiting for transfers between devices, gather_weight(): return lax.all_gather(shard, SHARD_AXES, axis=0, tiled=True)  75.1 us
    pallas_call x1, Pallas kernels, body(): pl.pallas_call(functools.partial(attn_fwd_kernel, scale), grid=(batch,),...  49.4 us
  transfers between devices with their start and end apart: 22, of which 9 were waited for; matrix products, arithmetic and copies ran while one was open for 28% of the time, Pallas kernels for 3%

profile of v2, /device:TPU:0, one launch (start us, length us, event | category | flops | bytes accessed | tf_op | source)
XLA Modules:
  0.0 2000.3 jit_solution(4740358948914653199)
XLA Ops:
  12.8 12.7 all-gather.1
  40.1 32.7 %all-gather.8.cloned.1.call-done = bf16[2048,2560]{0,1:T(8,128)(2,1)} async-done(((bf16[256,2560]{0,1:T(8,128)(2,1)}), bf16[2048,2560]{0,1:T(8,128)(2,1)}) %all-gather.8.cloned.1.call-update) | async-done | bytes 10485776 | tf_op jit(solution)/shard_map/all_gather | solution.py:171
  72.8 29.1 %fusion.96.kv_ref.q_ref = f32[2048,2560]{1,0:T(8,128)} fusion(bf16[2048,2048]{1,0:T(8,128)(2,1)} %fusion.17, bf16[2048,2560]{0,1:T(8,128)(2,1)} %all-gather.8.cloned.1.call-done), kind=kOutput, calls=%fused_computation.181 | convolution fusion | flops 21474836480 | bytes 39845888 | tf_op jit(solution)/shard_map/td,dn->tn/dot_general | solution.py:20
  108.3 77.9 %collective-permute-done.kvo_ref = bf16[2048,512]{1,0:T(8,128)(2,1)} collective-permute-done((bf16[2048,512]{1,0:T(8,128)(2,1)S(1)}, bf16[2048,512]{1,0:T(8,128)(2,1)}, u32[]{:S(2)}, u32[]{:S(2)}) %collective-permute-start) | collective-permute-done | bytes 2097184 | tf_op jit(solution)/shard_map/ppermute | solution.py:184
  186.2 49.4 %attn_fwd.1 = (bf16[2048,2048]{1,0:T(8,128)(2,1)}, bf16[2048,2048]{1,0:T(8,128)(2,1)}) custom-call(f32[2048,2560]{1,0:T(8,128)} %fusion.96.kv_ref.q_ref, bf16[2048,512]{1,0:T(8,128)(2,1)S(1)} %rope_kv.1.kv_ref, bf16[2048,512]{1,0:T(8,128)(2,1)} %collective-permute-done.kvo_ref, f32[256,128]{1,0:T(8,128)S(1)} %maximum_maximum_fusion.cos_ref, ...), custom_call_target="tpu_custom_call" | custom-call | flops 4294967296 | bytes 40000000 | tf_op jit(solution)/shard_map/attn_fwd/pallas_call | solution.py:277
  236.3 25.0 %fusion.11 = (f32[2048]{0:T(1024)S(1)}, bf16[2048,2048]{1,0:T(8,128)(2,1)}) fusion(bf16[2048,2048]{1,0:T(8,128)(2,1)} %get-tuple-element.48, bf16[2048,2048]{1,0:T(8,128)(2,1)} %all-gather.10.cloned.1.call-done, bf16[32,64,2048]{2,1,0:T(8,128)(2,1)} %param.12), kind=kOutput, calls=%fused_computation.20 | convolution fusion | flops 17205032960 | bytes 33562624 | tf_op jit(solution)/shard_map/tn,nd->td/dot_general | solution.py:20
  278.7 58.2 %fusion.97 = f32[2048,5632]{1,0:T(8,128)} fusion(bf16[2048,2048]{1,0:T(8,128)(2,1)} %fusion.5, bf16[2048,5632]{1,0:T(8,128)(2,1)} %all-gather.12.cloned.1.call-done), kind=kOutput, calls=%fused_computation.182 | convolution fusion | flops 47244640256 | bytes 77594624 | tf_op jit(solution)/shard_map/td,df->tf/dot_general | solution.py:20
  336.9 42.4 %all-gather.14.cloned.1.call-done = bf16[2048,5632]{1,0:T(8,128)(2,1)} async-done(((bf16[256,5632]{1,0:T(8,128)(2,1)}), bf16[2048,5632]{1,0:T(8,128)(2,1)}) %all-gather.14.cloned.1.call-update) | async-done | bytes 23068688 | tf_op jit(solution)/shard_map/all_gather | solution.py:171
  379.3 66.3 %multiply_convert_fusion.2 = (bf16[2048,5632]{1,0:T(8,128)(2,1)}, f32[2048,5632]{1,0:T(8,128)}) fusion(f32[2048,5632]{1,0:T(8,128)} %fusion.97, bf16[2048,2048]{1,0:T(8,128)(2,1)} %fusion.5, bf16[2048,5632]{1,0:T(8,128)(2,1)} %all-gather.14.cloned.1.call-done), kind=kOutput, calls=%fused_computation.2 | convolution fusion | flops 47313846272 | bytes 146800640 | tf_op jit(solution)/shard_map/td,df->tf/dot_general | solution.py:20
  445.6 58.4 %convolution_multiply_fusion = f32[5632,2048]{1,0:T(8,128)} fusion(bf16[2048,5632]{1,0:T(8,128)(2,1)} %get-tuple-element.64, bf16[2048,2048]{1,0:T(8,128)(2,1)} %bitcast.89), kind=kOutput, calls=%fused_computation.5 | convolution fusion | flops 47256174592 | bytes 77594624 | tf_op jit(solution)/shard_map/tf,td->fd/dot_general | solution.py:20
  504.0 85.4 %multiply_convert_fusion = (bf16[2048,5632]{1,0:T(8,128)(2,1)}, bf16[2048,5632]{1,0:T(8,128)(2,1)}) fusion(f32[2048,5632]{1,0:T(8,128)} %fusion.97, f32[2048,5632]{1,0:T(8,128)} %get-tuple-element.140, bf16[2048,2048]{1,0:T(8,128)(2,1)} %bitcast.90, bf16[5632,2048]{1,0:T(8,128)(2,1)} %all-gather.16.cloned.1.call-done), kind=kOutput, calls=%fused_computation | convolution fusion | flops 47394586624 | bytes 169869312 | tf_op jit(solution)/shard_map/td,fd->tf/dot_general | solution.py:20
  589.4 33.3 %convolution_multiply_fusion.2 = f32[1024,5632]{1,0:T(8,128)} fusion(bf16[2048,5632]{1,0:T(8,128)(2,1)} %get-tuple-element.55, bf16[2048,256]{1,0:T(8,128)(2,1)S(1)} %copy-done.32, bf16[2048,256]{1,0:T(8,128)(2,1)} %get-tuple-element.123, bf16[2048,256]{1,0:T(8,128)(2,1)} %get-tuple-element.124, bf16[2048,256]{1,0:T(8,128)(2,1)} %get-tuple-element.125), kind=kOutput, calls=%fused_computation.38 | convolution fusion | flops 23644864512 | bytes 50331648 | tf_op jit(solution)/shard_map/td,tn->dn/dot_general | solution.py:20
  626.3 59.4 %convolution_multiply_fusion.1 = f32[2048,5632]{1,0:T(8,128)} fusion(bf16[2048,2048]{1,0:T(8,128)(2,1)} %fusion.5, bf16[2048,5632]{1,0:T(8,128)(2,1)} %get-tuple-element.56), kind=kOutput, calls=%fused_computation.6 | convolution fusion | flops 47256174592 | bytes 77594624 | tf_op jit(solution)/shard_map/td,tf->df/dot_general | solution.py:20
  685.7 21.7 %slice_add_fusion = f32[512,5632]{1,0:T(8,128)} fusion(f32[1024,5632]{1,0:T(8,128)} %collective-permute-done.1, bf16[2048,5632]{1,0:T(8,128)(2,1)} %get-tuple-element.55, bf16[2048,256]{1,0:T(8,128)(2,1)} %get-tuple-element.121, bf16[2048,256]{1,0:T(8,128)(2,1)} %get-tuple-element.120), kind=kOutput, calls=%fused_computation.39 | convolution fusion | flops 11821121536 | bytes 48234496 | tf_op jit(solution)/shard_map/td,tn->dn/dot_general | solution.py:20
  707.4 21.3 %slice_add_fusion.1 = f32[512,5632]{1,0:T(8,128)} fusion(f32[1024,5632]{1,0:T(8,128)} %collective-permute-done.1, bf16[2048,5632]{1,0:T(8,128)(2,1)} %get-tuple-element.55, bf16[2048,256]{1,0:T(8,128)(2,1)S(1)} %copy-done.10, bf16[2048,256]{1,0:T(8,128)(2,1)} %get-tuple-element.127), kind=kOutput, calls=%fused_computation.40 | convolution fusion | flops 11821121536 | bytes 48234496 | tf_op jit(solution)/shard_map/td,tn->dn/dot_general | solution.py:20
  728.7 60.5 %fusion.98 = f32[2048,2048]{1,0:T(8,128)} fusion(bf16[2048,5632]{1,0:T(8,128)(2,1)} %get-tuple-element.55, bf16[2048,5632]{1,0:T(8,128)(2,1)} %all-gather.12.cloned.1.call-done), kind=kOutput, calls=%fused_computation.183 | convolution fusion | flops 47244640256 | bytes 62914560 | tf_op jit(solution)/shard_map/tf,df->td/dot_general | solution.py:20
  789.2 68.4 %fusion.10 = (f32[2048]{0:T(1024)}, f32[2048]{0:T(1024)S(1)}, f32[2048,2048]{1,0:T(8,128)}) fusion(bf16[2048,2048]{1,0:T(8,128)(2,1)} %get-tuple-element.138, f32[2048]{0:T(1024)S(1)} %copy-done.37, f32[2048]{0:T(1024)S(1)} %bitcast.101, f32[2048,2048]{1,0:T(8,128)} %fusion.98, bf16[2048,5632]{1,0:T(8,128)(2,1)} %get-tuple-element.56, ...), kind=kOutput, calls=%fused_computation.19 | convolution fusion | flops 47278194688 | bytes 88113152 | tf_op jit(solution)/shard_map/tf,df->td/dot_general | solution.py:20
  857.6 13.0 fusion.91
  870.7 12.4 convolution_multiply_fusion.3
  886.7 22.0 %convolution_convert_fusion.dc_ref = bf16[2048,2048]{1,0:T(8,128)(2,1)} fusion(bf16[2048,2048]{1,0:T(8,128)(2,1)S(1)} %fusion.91, bf16[2048,2048]{1,0:T(8,128)(2,1)} %all-gather.10.cloned.1.call-done), kind=kOutput, calls=%fused_computation.42 | convolution fusion | flops 17184063488 | bytes 25165824 | tf_op jit(solution)/shard_map/td,nd->tn/dot_general | solution.py:20
  916.7 10.3 slice_add_fusion.5
  927.0 88.7 %attn_bwd.1 = (bf16[2048,2560]{1,0:T(8,128)(2,1)}, f32[2048,512]{1,0:T(8,128)}, f32[2048,512]{1,0:T(8,128)}) custom-call(bf16[2048,2048]{1,0:T(8,128)(2,1)} %get-tuple-element.49.qb_ref, bf16[2048,2048]{1,0:T(8,128)(2,1)} %convolution_convert_fusion.dc_ref, bf16[2048,512]{1,0:T(8,128)(2,1)S(1)} %rope_kv.1.kv_ref, ...), custom_call_target="tpu_custom_call" | custom-call | flops 10737418240 | bytes 50000000 | tf_op jit(solution)/shard_map/attn_bwd/pallas_call | solution.py:321
  1039.1 69.4 %collective-permute-done.3.got_ref = f32[2048,512]{1,0:T(8,128)} collective-permute-done((f32[2048,512]{1,0:T(8,128)}, f32[2048,512]{1,0:T(8,128)}, u32[]{:S(2)}, u32[]{:S(2)}) %collective-permute-start.3) | collective-permute-done | bytes 4194336 | tf_op jit(solution)/shard_map/ppermute | solution.py:184
  1126.1 58.9 %fusion.12 = bf16[2048,2048]{1,0:T(8,128)(2,1)} fusion(bf16[2048,2048]{1,0:T(8,128)(2,1)} %get-tuple-element.138, bf16[2048,5632]{1,0:T(8,128)(2,1)} %get-tuple-element.64, bf16[5632,2048]{1,0:T(8,128)(2,1)} %all-gather.16.cloned.1.call-done), kind=kOutput, calls=%fused_computation.21 | convolution fusion | flops 47257223168 | bytes 62914560 | tf_op jit(solution)/shard_map/tf,fd->td/dot_general | solution.py:20
  1211.3 318.3 %collective-permute-done.12 = f32[512,5632]{1,0:T(8,128)} collective-permute-done((f32[512,5632]{1,0:T(8,128)}, f32[512,5632]{1,0:T(8,128)}, u32[]{:S(2)}, u32[]{:S(2)}) %collective-permute-start.12) | collective-permute-done | bytes 11534368 | tf_op jit(solution)/shard_map/ppermute | solution.py:184
  1538.2 128.4 %collective-permute-done.10 = f32[512,2048]{1,0:T(8,128)S(1)} collective-permute-done((f32[512,2048]{1,0:T(8,128)}, f32[512,2048]{1,0:T(8,128)S(1)}, u32[]{:S(2)}, u32[]{:S(2)}) %collective-permute-start.10) | collective-permute-done | bytes 4194336 | tf_op jit(solution)/shard_map/ppermute | solution.py:184
  1669.6 34.1 %fusion.23 = (f32[2048]{0:T(1024)S(1)}, f32[2048]{0:T(1024)S(1)}, f32[2048,2048]{1,0:T(8,128)}) fusion(bf16[32,64,2048]{2,1,0:T(8,128)(2,1)S(1)} %bitcast.86, f32[2048]{0:T(1024)S(1)} %copy-done.40, f32[2048]{0:T(1024)S(1)} %bitcast.105, bf16[2048,2560]{1,0:T(8,128)(2,1)} %unrope_kv.1, bf16[2048,2560]{0,1:T(8,128)(2,1)} %all-gather.8.cloned.1.call-done), kind=kOutput, calls=%fused_computation.35 | convolution fusion | flops 21504192512 | bytes 46170112 | tf_op jit(solution)/shard_map/tn,dn->td/dot_general | solution.py:20
  1703.7 23.0 %fusion.22 = bf16[2048,2048]{1,0:T(8,128)(2,1)} fusion(bf16[32,64,2048]{2,1,0:T(8,128)(2,1)S(1)} %bitcast.86, f32[2048,2048]{1,0:T(8,128)} %get-tuple-element.142, f32[2048]{0:T(1024)S(1)} %broadcast_multiply_fusion, f32[2048]{0:T(1024)S(1)} %bitcast.106, f32[2048]{0:T(1024)S(1)} %copy-done.40, bf16[2048,2048]{1,0:T(8,128)(2,1)} %bitcast.92, ...), kind=kLoop, calls=%fused_computation.34 | loop fusion | flops 67108864 | bytes 67158016 | tf_op jit(solution)/shard_map/convert_element_type | solution.py:362
  1726.7 165.3 %all-reduce.1 = f32[8,2,256]{2,1,0:T(2,128)S(1)} all-reduce(f32[8,2,256]{2,1,0:T(2,128)S(1)} %pad_maximum_fusion.30), channel_id=3, replica_groups=mesh['cp'=2,'fsdp'=4] {'fsdp','cp'}, use_global_device_ids=true, to_apply=%region_6.7.clone | all-reduce | flops 4096 | bytes 32768
  1905.0 17.0 collective-permute-done.7
  1923.5 16.6 collective-permute-done.9
  1956.7 36.6 %reduce-scatter.8.cloned.1.call-done = f32[704,2048]{1,0:T(8,128)} async-done(((f32[5632,2048]{1,0:T(8,128)}), f32[704,2048]{1,0:T(8,128)}) %reduce-scatter.8.cloned.1.call-update) | async-done | bytes 5767184 | tf_op jit(solution)/shard_map/reduce_scatter | solution.py:175
  (208 shorter events, 169.3 us)
Async XLA Ops:
  7.2 65.6 %all-gather.8.cloned.1.call-start = ((), (), s32[]{:S(2)}) async-start(), calls=%async_computation.3 | async-start | bytes 11796480 | tf_op jit(solution)/shard_map/all_gather | solution.py:171
  9.8 226.5 %all-gather.10.cloned.1.call-start = ((), (), s32[]{:S(2)}) async-start(), calls=%async_computation.4 | async-start | bytes 9437184 | tf_op jit(solution)/shard_map/all_gather | solution.py:171
  10.5 268.1 %all-gather.12.cloned.1.call-start = ((), (), s32[]{:S(2)}) async-start(), calls=%async_computation.5 | async-start | bytes 25952256 | tf_op jit(solution)/shard_map/all_gather | solution.py:171
  11.3 368.0 %all-gather.14.cloned.1.call-start = ((), (), s32[]{:S(2)}) async-start(), calls=%async_computation.6 | async-start | bytes 25952256 | tf_op jit(solution)/shard_map/all_gather | solution.py:171
  11.9 492.1 %all-gather.16.cloned.1.call-start = ((), (), s32[]{:S(2)}) async-start(), calls=%async_computation.7 | async-start | bytes 25952256 | tf_op jit(solution)/shard_map/all_gather | solution.py:171
  12.4 1941.4 %reduce-scatter.4.cloned.1.call-start = ((), (), s32[]{:S(2)}) async-start(), calls=%async_computation.8 | async-start | bytes 4718592 | tf_op jit(solution)/shard_map/reduce_scatter | solution.py:175
  25.5 235.8 %copy-start.33 = (f32[8,1,256]{2,1,0:T(1,128)}, f32[8,1,256]{2,1,0:T(1,128)S(1)}, u32[]{:S(2)}) copy-start(f32[8,1,256]{2,1,0:T(1,128)S(1)} %get-tuple-element.130) | copy-start | bytes 24580
  107.4 78.8 %collective-permute-start = (bf16[2048,512]{1,0:T(8,128)(2,1)S(1)}, bf16[2048,512]{1,0:T(8,128)(2,1)}, u32[]{:S(2)}, u32[]{:S(2)}) collective-permute-start(bf16[2048,512]{1,0:T(8,128)(2,1)S(1)} %rope_kv.1.kv_ref), channel_id=1, source_target_pairs={{0,4},{4,0},{1,5},{5,1},{2,6},{6,2},{3,7},{7,3}} | collective-permute-start | bytes 6291464 | tf_op jit(solution)/shard_map/ppermute | solution.py:184
  108.0 78.2 %copy-start.3 = (f32[256,128]{1,0:T(8,128)}, f32[256,128]{1,0:T(8,128)S(1)}, u32[]{:S(2)}) copy-start(f32[256,128]{1,0:T(8,128)S(1)} %maximum_maximum_fusion.1.sin_ref) | copy-start | bytes 393220
  108.2 78.0 %copy-start.1 = (f32[256,128]{1,0:T(8,128)}, f32[256,128]{1,0:T(8,128)S(1)}, u32[]{:S(2)}) copy-start(f32[256,128]{1,0:T(8,128)S(1)} %maximum_maximum_fusion.cos_ref) | copy-start | bytes 393220
  504.0 85.4 %copy-start.32 = (bf16[2048,256]{1,0:T(8,128)(2,1)S(1)}, bf16[2048,256]{1,0:T(8,128)(2,1)}, u32[]{:S(2)}) copy-start(bf16[2048,256]{1,0:T(8,128)(2,1)} %get-tuple-element.122) | copy-start | bytes 3145732
  622.7 63.0 %collective-permute-start.1 = (f32[1024,5632]{1,0:T(8,128)}, f32[1024,5632]{1,0:T(8,128)}, u32[]{:S(2)}, u32[]{:S(2)}) collective-permute-start(f32[1024,5632]{1,0:T(8,128)} %convolution_multiply_fusion.2), channel_id=1, source_target_pairs={{0,1},{1,0},{2,3},{3,2},{4,5},{5,4},{6,7},{7,6}} | collective-permute-start | bytes 69206024 | tf_op jit(solution)/shard_map/ppermute | solution.py:184
  883.1 25.6 %collective-permute-start.2 = (f32[1024,2048]{1,0:T(8,128)}, f32[1024,2048]{1,0:T(8,128)}, u32[]{:S(2)}, u32[]{:S(2)}) collective-permute-start(f32[1024,2048]{1,0:T(8,128)} %convolution_multiply_fusion.3), channel_id=1, source_target_pairs={{0,1},{1,0},{2,3},{3,2},{4,5},{5,4},{6,7},{7,6}} | collective-permute-start | bytes 25165832 | tf_op jit(solution)/shard_map/ppermute | solution.py:184
  1015.7 92.9 %collective-permute-start.3 = (f32[2048,512]{1,0:T(8,128)}, f32[2048,512]{1,0:T(8,128)}, u32[]{:S(2)}, u32[]{:S(2)}) collective-permute-start(f32[2048,512]{1,0:T(8,128)} %get-tuple-element.67), channel_id=1, source_target_pairs={{0,4},{4,0},{1,5},{5,1},{2,6},{6,2},{3,7},{7,3}} | collective-permute-start | bytes 12582920 | tf_op jit(solution)/shard_map/ppermute | solution.py:184
  1032.5 76.0 %copy-start = (f32[2048,512]{1,0:T(8,128)S(1)}, f32[2048,512]{1,0:T(8,128)}, u32[]{:S(2)}) copy-start(f32[2048,512]{1,0:T(8,128)} %get-tuple-element.66.own_ref) | copy-start | bytes 12582916
  1123.1 833.5 %reduce-scatter.6.cloned.1.call-start = ((), (), s32[]{:S(2)}) async-start(), calls=%async_computation.9 | async-start | bytes 51904512 | tf_op jit(solution)/shard_map/reduce_scatter | solution.py:175
  1123.9 869.3 %reduce-scatter.8.cloned.1.call-start = ((), (), s32[]{:S(2)}) async-start(), calls=%async_computation.10 | async-start | bytes 51904512 | tf_op jit(solution)/shard_map/reduce_scatter | solution.py:175
  1125.3 404.4 %collective-permute-start.12 = (f32[512,5632]{1,0:T(8,128)}, f32[512,5632]{1,0:T(8,128)}, u32[]{:S(2)}, u32[]{:S(2)}) collective-permute-start(f32[512,5632]{1,0:T(8,128)} %slice_add_fusion.1), channel_id=1, source_target_pairs={{0,4},{4,0},{1,5},{5,1},{2,6},{6,2},{3,7},{7,3}} | collective-permute-start | bytes 34603016 | tf_op jit(solution)/shard_map/ppermute | solution.py:184
  1125.5 61.1 %collective-permute-start.5 = (f32[1024,1024]{1,0:T(8,128)}, f32[1024,1024]{1,0:T(8,128)}, u32[]{:S(2)}, u32[]{:S(2)}) collective-permute-start(f32[1024,1024]{1,0:T(8,128)} %fusion.49), channel_id=1, source_target_pairs={{0,1},{1,0},{2,3},{3,2},{4,5},{5,4},{6,7},{7,6}} | collective-permute-start | bytes 12582920 | tf_op jit(solution)/shard_map/ppermute | solution.py:184
  1125.6 74.0 %collective-permute-start.4 = (f32[1024,1024]{1,0:T(8,128)}, f32[1024,1024]{1,0:T(8,128)}, u32[]{:S(2)}, u32[]{:S(2)}) collective-permute-start(f32[1024,1024]{1,0:T(8,128)} %fusion.50), channel_id=1, source_target_pairs={{0,1},{1,0},{2,3},{3,2},{4,5},{5,4},{6,7},{7,6}} | collective-permute-start | bytes 12582920 | tf_op jit(solution)/shard_map/ppermute | solution.py:184
  1184.9 481.7 %collective-permute-start.10 = (f32[512,2048]{1,0:T(8,128)}, f32[512,2048]{1,0:T(8,128)S(1)}, u32[]{:S(2)}, u32[]{:S(2)}) collective-permute-start(f32[512,2048]{1,0:T(8,128)} %slice_add_fusion.5), channel_id=1, source_target_pairs={{0,4},{4,0},{1,5},{5,1},{2,6},{6,2},{3,7},{7,3}} | collective-permute-start | bytes 12582920 | tf_op jit(solution)/shard_map/ppermute | solution.py:184
  1205.3 464.3 %slice-start = ((s8[8388608]{0:T(1024)(128)(4,1)}), s8[4194304]{0:T(1024)(128)(4,1)S(1)}, s32[]{:S(2)}) async-start(s8[8388608]{0:T(1024)(128)(4,1)} %bitcast.85), calls=%async_computation.11 | async-start | bytes 8388608
  1211.3 455.3 %copy-start.11 = (f32[512,2048]{1,0:T(8,128)S(1)}, f32[512,2048]{1,0:T(8,128)}, u32[]{:S(2)}) copy-start(f32[512,2048]{1,0:T(8,128)} %slice_add_fusion.4) | copy-start | bytes 12582916
  1211.3 458.3 %slice-start.1 = ((s8[8388608]{0:T(1024)(128)(4,1)}), s8[4194304]{0:T(1024)(128)(4,1)S(1)}, s32[]{:S(2)}) async-start(s8[8388608]{0:T(1024)(128)(4,1)} %bitcast.85), calls=%async_computation.12 | async-start | bytes 8388608
  1211.3 458.3 %copy-start.40 = (f32[2048]{0:T(1024)S(1)}, f32[2048]{0:T(1024)}, u32[]{:S(2)}) copy-start(f32[2048]{0:T(1024)} %copy-done.39) | copy-start | bytes 24580
  1211.3 458.3 %copy-start.42 = (f32[8,1,256]{2,1,0:T(1,128)S(1)}, f32[8,1,256]{2,1,0:T(1,128)}, u32[]{:S(2)}) copy-start(f32[8,1,256]{2,1,0:T(1,128)} %copy-done.41) | copy-start | bytes 24580
  1537.1 406.4 %collective-permute-start.13 = (f32[256,5632]{1,0:T(8,128)}, f32[256,5632]{1,0:T(8,128)}, u32[]{:S(2)}, u32[]{:S(2)}) collective-permute-start(f32[256,5632]{1,0:T(8,128)} %slice_add_fusion.2), channel_id=1, source_target_pairs={{0,2},{2,0},{1,3},{3,1},{4,6},{6,4},{5,7},{7,5}} | collective-permute-start | bytes 17301512 | tf_op jit(solution)/shard_map/ppermute | solution.py:184
  1666.9 233.1 %collective-permute-start.11 = (f32[256,2048]{1,0:T(8,128)S(1)}, f32[256,2048]{1,0:T(8,128)}, u32[]{:S(2)}, u32[]{:S(2)}) collective-permute-start(f32[256,2048]{1,0:T(8,128)S(1)} %slice_add_fusion.6), channel_id=1, source_target_pairs={{0,2},{2,0},{1,3},{3,1},{4,6},{6,4},{5,7},{7,5}} | collective-permute-start | bytes 6291464 | tf_op jit(solution)/shard_map/ppermute | solution.py:184
  1668.5 224.3 %collective-permute-start.6 = (f32[512,1024]{1,0:T(8,128)}, f32[512,1024]{1,0:T(8,128)}, u32[]{:S(2)}, u32[]{:S(2)}) collective-permute-start(f32[512,1024]{1,0:T(8,128)} %slice_add_fusion.11), channel_id=1, source_target_pairs={{0,2},{2,0},{1,3},{3,1},{4,6},{6,4},{5,7},{7,5}} | collective-permute-start | bytes 6291464 | tf_op jit(solution)/shard_map/ppermute | solution.py:184
  1669.0 228.0 %collective-permute-start.8 = (f32[512,1024]{1,0:T(8,128)}, f32[512,1024]{1,0:T(8,128)}, u32[]{:S(2)}, u32[]{:S(2)}) collective-permute-start(f32[512,1024]{1,0:T(8,128)} %slice_add_fusion.9), channel_id=1, source_target_pairs={{0,4},{4,0},{1,5},{5,1},{2,6},{6,2},{3,7},{7,3}} | collective-permute-start | bytes 6291464 | tf_op jit(solution)/shard_map/ppermute | solution.py:184
  1894.8 27.2 %collective-permute-start.7 = (f32[256,1024]{1,0:T(8,128)S(1)}, f32[256,1024]{1,0:T(8,128)S(1)}, u32[]{:S(2)}, u32[]{:S(2)}) collective-permute-start(f32[256,1024]{1,0:T(8,128)S(1)} %slice_add_fusion.14), channel_id=1, source_target_pairs={{0,4},{4,0},{1,5},{5,1},{2,6},{6,2},{3,7},{7,3}} | collective-permute-start | bytes 3145736 | tf_op jit(solution)/shard_map/ppermute | solution.py:184
  1898.7 41.4 %collective-permute-start.9 = (f32[256,1024]{1,0:T(8,128)S(1)}, f32[256,1024]{1,0:T(8,128)S(1)}, u32[]{:S(2)}, u32[]{:S(2)}) collective-permute-start(f32[256,1024]{1,0:T(8,128)S(1)} %slice_add_fusion.12), channel_id=1, source_target_pairs={{0,2},{2,0},{1,3},{3,1},{4,6},{6,4},{5,7},{7,5}} | collective-permute-start | bytes 3145736 | tf_op jit(solution)/shard_map/ppermute | solution.py:184
  (44 other events, 898.8 us)
Sparse Core Ops, SparseCore 0:
  10.4 62.3 all-gather.7
  74.7 59.8 all-gather.9
  136.4 130.3 all-gather.11
  268.5 110.7 all-gather.13
  380.9 110.7 all-gather.15
  1123.3 59.6 reduce-scatter.3
  1187.1 442.0 reduce-scatter.5
  1633.3 359.9 reduce-scatter.7

commit v3 on v1

--- a/solution.py
+++ b/solution.py
@@ -175,6 +175,57 @@
     return lax.psum_scatter(local_grad, SHARD_AXES, scatter_dimension=0, tiled=True)
 
 
+SWAP_CORE = ("fsdp", [(0, 1), (1, 0), (2, 3), (3, 2)])
+SWAP_X = ("fsdp", [(0, 2), (2, 0), (1, 3), (3, 1)])
+SWAP_Y = ("cp", [(0, 1), (1, 0)])
+
+
+def swap(vals, how):
+    return lax.ppermute(vals, how[0], how[1])
+
+
+def place():
+    at = lax.axis_index("fsdp")
+    return at // 2, at % 2, lax.axis_index("cp")
+
+
+def relative_blocks(lhs):
+    block = lhs.shape[1] // 8
+    x_at, core, y_at = place()
+    sides = []
+    for d_core in (0, 1):
+        parts = []
+        for d_y in (0, 1):
+            for d_x in (0, 1):
+                owner = (((x_at + d_x) % 2) * 2 + (core + d_core) % 2) * 2 + (y_at + d_y) % 2
+                parts.append(lax.dynamic_slice_in_dim(lhs, owner * block + block // 2, block // 2, 1))
+        sides.append(parts)
+    return sides
+
+
+def first_halves(lhs):
+    block = lhs.shape[1] // 8
+    return jnp.concatenate([lhs[:, i * block:i * block + block // 2] for i in range(8)], axis=1)
+
+
+def core_blocks(lhs, d_core):
+    block = lhs.shape[1] // 4
+    x_at, core, _ = place()
+    starts = [(((x_at + d_x) % 2) * 2 + (core + d_core) % 2) * block for d_x in (0, 1)]
+    return jnp.concatenate([lax.dynamic_slice_in_dim(lhs, at, block, 1) for at in starts], axis=1)
+
+
+def partner_part(blocks, rhs, scale):
+    return matmul("td,tn->dn", jnp.concatenate(blocks[1], axis=1), rhs) * scale
+
+
+def own_parts(blocks, rhs, got, scale):
+    cut = got.shape[0] // 2
+    far = matmul("td,tn->dn", jnp.concatenate(blocks[0][2:], axis=1), rhs) * scale + got[cut:]
+    near = matmul("td,tn->dn", jnp.concatenate(blocks[0][:2], axis=1), rhs) * scale + got[:cut]
+    return far, near
+
+
 def solution(mesh):
     n_dev = mesh.shape["fsdp"] * mesh.shape["cp"]
     act_spec = P("fsdp", "cp", None)
@@ -191,6 +242,7 @@
         q_cols, kv_cols = heads * head_dim, kv_heads * head_dim
         tokens = batch * seq
         scale = head_dim ** -0.5
+        share = 1.0 / n_dev
         x = act_in.reshape(tokens, width)
         dy = grad_out.reshape(tokens, width)
 
@@ -236,8 +288,7 @@
             out_shape=jax.ShapeDtypeStruct((tokens, 2 * kv_cols), bf16),
             compiler_params=params(), cost_estimate=cost(1e9, 6e6), name="rope_kv",
         )(qkv, cos_t, sin_t)
-        swap = [(0, 1), (1, 0)]
-        kv_oth = lax.ppermute(kv, "cp", swap)
+        kv_oth = swap(kv, SWAP_Y)
         ctx, query = pl.pallas_call(
             functools.partial(attn_fwd_kernel, scale), grid=(batch,),
             in_specs=[q_blk, kv_blk, kv_blk, whole(cos_4), whole(sin_4), whole(mask_4)],
@@ -247,33 +298,61 @@
         )(qkv, kv, kv_oth, cos_4, sin_4, mask_4)
         resid = (x.astype(f32) + matmul("tn,nd->td", ctx, full_o)).astype(bf16)
         normed2, rms2 = norm_fwd(resid, gain2)
+        normed2, blocks2, lhs_a = lax.optimization_barrier((normed2, relative_blocks(normed2), first_halves(normed2)))
         gate_pre = matmul("td,df->tf", normed2, full_gate)
         up_pre = matmul("td,df->tf", normed2, full_up)
         gate_sig = jax.nn.sigmoid(gate_pre)
         gate_act = gate_pre * gate_sig
         hidden = (gate_act * up_pre).astype(bf16)
 
-        grad_down = matmul("tf,td->fd", hidden, dy)
-        grad_down, dy, hidden = lax.optimization_barrier((grad_down, dy, hidden))
-        grad_down = scatter_grad(grad_down) / n_dev
+        half_w = width // 2
+        down_oth = matmul("tf,td->fd", core_blocks(hidden, 1), dy[:, half_w:]) * share
+        down_oth, hidden, dy = lax.optimization_barrier((down_oth, hidden, dy))
+        down_got = swap(down_oth, SWAP_CORE)
+        down_a = matmul("tf,td->fd", hidden, dy[:, :half_w]) * share
+        down_a, hidden, dy = lax.optimization_barrier((down_a, hidden, dy))
+        down_a = scatter_grad(down_a)
+        down_own = matmul("tf,td->fd", core_blocks(hidden, 0), dy[:, half_w:]) * share + down_got
+        down_own, hidden, dy = lax.optimization_barrier((down_own, hidden, dy))
+        y_at = place()[2]
+        down_own = down_own.reshape(2, 2, down_own.shape[0] // 4, half_w)
+        down_far = lax.dynamic_slice_in_dim(down_own, 1 - y_at, 1, 1)
+        down_far, dy = lax.optimization_barrier((down_far, dy))
+        down_got = swap(down_far, SWAP_Y)
         d_hidden = matmul("td,fd->tf", dy, full_down)
         d_gate = (d_hidden * up_pre * gate_sig * (1.0 + gate_pre * (1.0 - gate_sig))).astype(bf16)
         d_up = (d_hidden * gate_act).astype(bf16)
-        grad_gate = matmul("td,tf->df", normed2, d_gate)
-        grad_gate, d_up = lax.optimization_barrier((grad_gate, d_up))
-        grad_gate = scatter_grad(grad_gate) / n_dev
-        grad_up = matmul("td,tf->df", normed2, d_up)
-        grad_up, d_gate, d_up, hidden = lax.optimization_barrier((grad_up, d_gate, d_up, hidden))
-        grad_up = scatter_grad(grad_up) / n_dev
+
+        def split_grad(d_pre, after):
+            oth = partner_part(blocks2, d_pre, share)
+            oth, d_pre = lax.optimization_barrier((oth, d_pre))
+            got = swap(oth, SWAP_CORE)
+            whole_a = matmul("td,tn->dn", lhs_a, d_pre) * share
+            whole_a, d_pre = lax.optimization_barrier((whole_a, d_pre))
+            whole_a = scatter_grad(whole_a)
+            far, near = own_parts(blocks2, d_pre, got, share)
+            far, near, d_pre, after = lax.optimization_barrier((far, near, d_pre, after))
+            got = swap(far, SWAP_Y)
+            return whole_a, near, got, d_pre, after
+
+        gate_a, gate_near, gate_got, d_gate, d_up = split_grad(d_gate, d_up)
+        up_a, up_near, up_got, d_up, (d_gate, down_own) = split_grad(d_up, (d_gate, down_own))
+        down_near = lax.dynamic_slice_in_dim(down_own, y_at, 1, 1)
+        down_send = down_near[1] + down_got[1]
+        down_last = swap(down_send, SWAP_X)
         d_normed2 = matmul("tf,df->td", d_gate, full_gate)
         d_normed2 = d_normed2 + matmul("tf,df->td", d_up, full_up)
         d_resid, grad_ffn = norm_bwd(d_normed2, resid, rms2, gain2)
         d_resid = d_resid + dy.astype(f32)
         d_resid_half = d_resid.astype(bf16)
-        grad_o = matmul("tn,td->nd", ctx, d_resid_half)
+        grad_o = matmul("tn,td->nd", ctx, d_resid_half) * share
         grad_o, d_resid_half = lax.optimization_barrier((grad_o, d_resid_half))
-        grad_o = scatter_grad(grad_o) / n_dev
+        grad_o = scatter_grad(grad_o)
         d_ctx = matmul("td,nd->tn", d_resid_half, full_o).astype(bf16)
+        d_ctx, gate_near = lax.optimization_barrier((d_ctx, gate_near))
+        cut = rows // 2
+        gate_send = gate_near[cut:] + gate_got[cut:]
+        gate_last = swap(gate_send, SWAP_X)
         dq_wide, dkv_own, dkv_oth = pl.pallas_call(
             functools.partial(attn_bwd_kernel, scale), grid=(batch,),
             in_specs=[q_blk, q_blk, kv_blk, kv_blk, whole(cos_4), whole(sin_4), whole(mask_4)],
@@ -282,8 +361,15 @@
             + [jax.ShapeDtypeStruct((tokens, 2 * kv_cols), f32)] * 2,
             compiler_params=params(), cost_estimate=cost(10 * pair_flops, 50e6), name="attn_bwd",
         )(query, d_ctx, kv, kv_oth, cos_4, sin_4, mask_4)
-        dkv_got = lax.ppermute(dkv_oth, "cp", swap)
+        dkv_got = swap(dkv_oth, SWAP_Y)
+        grad_q = matmul("td,tn->dn", normed, dq_wide[:, :q_cols]) * share
+        grad_q, hidden = lax.optimization_barrier((grad_q, hidden))
+        grad_q = scatter_grad(grad_q)
         act_out = (resid.astype(f32) + matmul("tf,fd->td", hidden, full_down)).astype(bf16)
+        act_out, up_near = lax.optimization_barrier((act_out, up_near))
+        up_send = up_near[cut:] + up_got[cut:]
+        up_send, dkv_own = lax.optimization_barrier((up_send, dkv_own))
+        up_last = swap(up_send, SWAP_X)
         d_qkv = pl.pallas_call(
             unrope_kv_kernel, grid=(tokens // t_blk,),
             in_specs=[kv_tall, kv_tall, whole(cos_t), whole(sin_t), pl.BlockSpec(memory_space=pl.ANY)],
@@ -292,17 +378,20 @@
             input_output_aliases={4: 0},
             compiler_params=params(), cost_estimate=cost(1e9, 10e6), name="unrope_kv",
         )(dkv_own, dkv_got, cos_t, sin_t, dq_wide)
-        grad_qkv = matmul("td,tn->dn", normed, d_qkv)
-        grad_qkv, d_qkv = lax.optimization_barrier((grad_qkv, d_qkv))
-        grad_qkv = scatter_grad(grad_qkv) / n_dev
+        grad_kv = matmul("td,tn->dn", normed, d_qkv[:, q_cols:]) * share
+        grad_kv, d_qkv = lax.optimization_barrier((grad_kv, d_qkv))
+        grad_kv = scatter_grad(grad_kv)
         d_normed = matmul("tn,dn->td", d_qkv, full_qkv)
         d_input, grad_attn = norm_bwd(d_normed, x, rms1, gain1)
         grad_in = (d_resid + d_input).astype(bf16)
         gains = jnp.stack([grad_attn.reshape(n_dev, rows), grad_ffn.reshape(n_dev, rows)], axis=1)
-        gains = lax.psum_scatter(gains, SHARD_AXES, scatter_dimension=0, tiled=True)[0] / n_dev
-        grad_q = grad_qkv[:, :q_cols].reshape(w_q.shape)
-        grad_k = grad_qkv[:, q_cols:q_cols + kv_cols].reshape(w_k.shape)
-        grad_v = grad_qkv[:, q_cols + kv_cols:].reshape(w_v.shape)
+        gains = lax.psum_scatter(gains, SHARD_AXES, scatter_dimension=0, tiled=True)[0] * share
+        grad_down = jnp.concatenate([down_a, (down_near[0] + down_got[0] + down_last)[0]], axis=1)
+        grad_gate = jnp.concatenate([gate_a, gate_near[:cut] + gate_got[:cut] + gate_last], axis=0)
+        grad_up = jnp.concatenate([up_a, up_near[:cut] + up_got[:cut] + up_last], axis=0)
+        grad_q = grad_q.reshape(w_q.shape)
+        grad_k = grad_kv[:, :kv_cols].reshape(w_k.shape)
+        grad_v = grad_kv[:, kv_cols:].reshape(w_v.shape)
         shape = act_in.shape
         return (act_out.reshape(shape), grad_in.reshape(shape), gains[0], grad_q, grad_k, grad_v, grad_o, gains[1],
                 grad_gate, grad_up, grad_down)

time: 2050 us -> 1900 us (0.927)
  waiting for transfers between devices: 1000 us -> 603 us
  blocking collectives: 37.1 us -> 115 us
  matrix products: 738 us -> 815 us
  local copies, waits for them, and re-layouts: 16.1 us -> 65.7 us
  other arithmetic: 83.6 us -> 114 us
    reduce_scatter x5 -> x6, waiting for transfers between devices: 737 us -> 0.01 us  [scatter_grad(): lax.psum_scatter(local_grad, SHARD_AXES, scatter_dimension=0, tiled=True)]
    ppermute x2 -> x11, waiting for transfers between devices: 170 us -> 534 us  [swap(): return lax.ppermute(vals, how[0], how[1])]
    unnamed x1, blocking collectives: 23.8 us -> 102 us
    dot_general x15 -> x24, matrix products: 738 us -> 815 us  [matmul(): return jnp.einsum(form, lhs, rhs, preferred_element_type=jnp.float32)]
    dynamic_slice x0 -> x3, local copies, waits for them, and re-layouts: none -> 28.6 us  [the longest x2 22.6 us: core_blocks(): lax.dynamic_slice_in_dim(lhs, at, block, 1)]
    add x0 -> x5, other arithmetic: none -> 27.1 us  [the longest x1 6.77 us: body(): gate_near[:cut] + gate_got[:cut] + gate_last]
    div x6 -> x0, other arithmetic: 24.3 us -> none  [the longest x1 6.15 us: body(): grad_down = scatter_grad(grad_down) / n_dev]
    all_gather x5, waiting for transfers between devices: 89.7 us -> 65.5 us  [gather_weight(): return lax.all_gather(shard, SHARD_AXES, axis=0, tiled=True)]
  transfers between devices with their start and end apart: 12 -> 22, of which waited for: 8 -> 7; matrix products, arithmetic and copies ran while one was open for 22% -> 52% of each run, Pallas kernels for 7% -> 8%
where the time goes in v3:
time: 1900 us; the launch traced here: 1890 us
  matrix products  815 us (43%)
  waiting for transfers between devices  603 us (32%)
  Pallas kernels  150 us (8%)
  blocking collectives  115 us (6%)
  other arithmetic  114 us (6%)
  local copies, waits for them, and re-layouts  65.7 us (3%)
    dot_general x24, matrix products, matmul(): return jnp.einsum(form, lhs, rhs, preferred_element_type=jnp.float32)  815 us
    ppermute x11, waiting for transfers between devices, swap(): return lax.ppermute(vals, how[0], how[1])  534 us
    unnamed x1, blocking collectives  102 us
    pallas_call x1, Pallas kernels, body(): pl.pallas_call(functools.partial(attn_bwd_kernel, scale), grid=(batch,),...  88.7 us
    all_gather x5, waiting for transfers between devices, gather_weight(): return lax.all_gather(shard, SHARD_AXES, axis=0, tiled=True)  65.5 us
    pallas_call x1, Pallas kernels, body(): pl.pallas_call(functools.partial(attn_fwd_kernel, scale), grid=(batch,),...  49.4 us
  transfers between devices with their start and end apart: 22, of which 7 were waited for; matrix products, arithmetic and copies ran while one was open for 52% of the time, Pallas kernels for 8%

profile of v3, /device:TPU:0, one launch (start us, length us, event | category | flops | bytes accessed | tf_op | source)
XLA Modules:
  0.0 1889.9 jit_solution(7670534032258299649)
XLA Ops:
  40.4 32.6 %all-gather.8.cloned.1.call-done = bf16[2048,2560]{0,1:T(8,128)(2,1)} async-done(((bf16[256,2560]{0,1:T(8,128)(2,1)}), bf16[2048,2560]{0,1:T(8,128)(2,1)}) %all-gather.8.cloned.1.call-update) | async-done | bytes 10485776 | tf_op jit(solution)/shard_map/all_gather | solution.py:171
  72.9 29.1 %fusion.58.kv_ref.q_ref = f32[2048,2560]{1,0:T(8,128)} fusion(bf16[2048,2048]{1,0:T(8,128)(2,1)} %fusion.17, bf16[2048,2560]{0,1:T(8,128)(2,1)} %all-gather.8.cloned.1.call-done), kind=kOutput, calls=%fused_computation.140 | convolution fusion | flops 21474836480 | bytes 39845888 | tf_op jit(solution)/shard_map/td,dn->tn/dot_general | solution.py:20
  109.1 77.2 %collective-permute-done.kvo_ref = bf16[2048,512]{1,0:T(8,128)(2,1)} collective-permute-done((bf16[2048,512]{1,0:T(8,128)(2,1)S(1)}, bf16[2048,512]{1,0:T(8,128)(2,1)}, u32[]{:S(2)}, u32[]{:S(2)}) %collective-permute-start) | collective-permute-done | bytes 2097184 | tf_op jit(solution)/shard_map/ppermute | solution.py:184
  186.2 49.4 %attn_fwd.1 = (bf16[2048,2048]{1,0:T(8,128)(2,1)}, bf16[2048,2048]{1,0:T(8,128)(2,1)}) custom-call(f32[2048,2560]{1,0:T(8,128)} %fusion.58.kv_ref.q_ref, bf16[2048,512]{1,0:T(8,128)(2,1)S(1)} %rope_kv.1.kv_ref, bf16[2048,512]{1,0:T(8,128)(2,1)} %collective-permute-done.kvo_ref, f32[256,128]{1,0:T(8,128)S(1)} %maximum_maximum_fusion.cos_ref, ...), custom_call_target="tpu_custom_call" | custom-call | flops 4294967296 | bytes 40000000 | tf_op jit(solution)/shard_map/attn_fwd/pallas_call | solution.py:292
  236.4 24.6 %fusion.11 = (f32[2048]{0:T(1024)S(1)}, bf16[2048,2048]{1,0:T(8,128)(2,1)}) fusion(bf16[2048,2048]{1,0:T(8,128)(2,1)} %get-tuple-element.66, bf16[2048,2048]{1,0:T(8,128)(2,1)} %all-gather.10.cloned.1.call-done, bf16[32,64,2048]{2,1,0:T(8,128)(2,1)} %param.12), kind=kOutput, calls=%fused_computation.18 | convolution fusion | flops 17205032960 | bytes 33562624 | tf_op jit(solution)/shard_map/tn,nd->td/dot_general | solution.py:20
  287.9 58.5 %fusion.59 = f32[2048,5632]{1,0:T(8,128)} fusion(bf16[2048,2048]{1,0:T(8,128)(2,1)} %fusion.5, bf16[2048,5632]{1,0:T(8,128)(2,1)} %all-gather.12.cloned.1.call-done), kind=kOutput, calls=%fused_computation.141 | convolution fusion | flops 47244640256 | bytes 77594624 | tf_op jit(solution)/shard_map/td,df->tf/dot_general | solution.py:20
  346.4 33.0 %all-gather.14.cloned.1.call-done = bf16[2048,5632]{1,0:T(8,128)(2,1)} async-done(((bf16[256,5632]{1,0:T(8,128)(2,1)}), bf16[2048,5632]{1,0:T(8,128)(2,1)}) %all-gather.14.cloned.1.call-update) | async-done | bytes 23068688 | tf_op jit(solution)/shard_map/all_gather | solution.py:171
  379.4 66.7 %multiply_convert_fusion.2 = (bf16[2048,5632]{1,0:T(8,128)(2,1)}, f32[2048,5632]{1,0:T(8,128)}) fusion(f32[2048,5632]{1,0:T(8,128)} %fusion.59, bf16[2048,2048]{1,0:T(8,128)(2,1)} %fusion.5, bf16[2048,5632]{1,0:T(8,128)(2,1)} %all-gather.14.cloned.1.call-done), kind=kOutput, calls=%fused_computation.2 | convolution fusion | flops 47313846272 | bytes 146800640 | tf_op jit(solution)/shard_map/td,df->tf/dot_general | solution.py:20
  455.7 19.1 %fusion.37 = f32[2816,1024]{1,0:T(8,128)} fusion(bf16[2048,1408]{1,0:T(8,128)(2,1)} %get-tuple-element.141, bf16[2048,1408]{1,0:T(8,128)(2,1)} %get-tuple-element.140, bf16[2048,2048]{1,0:T(8,128)(2,1)} %bitcast.104), kind=kOutput, calls=%fused_computation.59 | convolution fusion | flops 11837112320 | bytes 27262976 | tf_op jit(solution)/shard_map/tf,td->fd/dot_general | solution.py:20
  480.7 31.7 %convolution_multiply_fusion = f32[5632,1024]{1,0:T(8,128)} fusion(bf16[2048,5632]{1,0:T(8,128)(2,1)} %get-tuple-element.101, bf16[2048,2048]{1,0:T(8,128)(2,1)} %bitcast.105), kind=kOutput, calls=%fused_computation.36 | convolution fusion | flops 23628087296 | bytes 50331648 | tf_op jit(solution)/shard_map/tf,td->fd/dot_general | solution.py:20
  525.4 26.1 %multiply_add_fusion = f32[2816,1024]{1,0:T(8,128)} fusion(f32[2816,1024]{1,0:T(8,128)} %collective-permute-done.1, bf16[2048,1408]{1,0:T(8,128)(2,1)} %get-tuple-element.139, bf16[2048,1408]{1,0:T(8,128)(2,1)} %get-tuple-element.138, bf16[2048,2048]{1,0:T(8,128)(2,1)} %bitcast.106), kind=kOutput, calls=%fused_computation.47 | convolution fusion | flops 11839995904 | bytes 38797312 | tf_op jit(solution)/shard_map/tf,td->fd/dot_general | solution.py:20
  557.6 85.8 %multiply_convert_fusion = (bf16[2048,5632]{1,0:T(8,128)(2,1)}, bf16[2048,5632]{1,0:T(8,128)(2,1)}) fusion(f32[2048,5632]{1,0:T(8,128)} %fusion.59, f32[2048,5632]{1,0:T(8,128)} %get-tuple-element.163, bf16[2048,2048]{1,0:T(8,128)(2,1)} %bitcast.107, bf16[5632,2048]{1,0:T(8,128)(2,1)} %all-gather.16.cloned.1.call-done), kind=kOutput, calls=%fused_computation | convolution fusion | flops 47394586624 | bytes 169869312 | tf_op jit(solution)/shard_map/td,fd->tf/dot_general | solution.py:20
  643.4 20.3 %convolution_multiply_fusion.4 = f32[512,5632]{1,0:T(8,128)} fusion(bf16[2048,512]{1,0:T(8,128)(2,1)} %constant_dynamic-update-slice_fusion.2, bf16[2048,5632]{1,0:T(8,128)(2,1)} %get-tuple-element.94), kind=kOutput, calls=%fused_computation.49 | convolution fusion | flops 11814043648 | bytes 36700160 | tf_op jit(solution)/shard_map/td,tn->dn/dot_general | solution.py:20
  665.6 35.0 %convolution_multiply_fusion.2 = f32[1024,5632]{1,0:T(8,128)} fusion(bf16[2048,1024]{1,0:T(8,128)(2,1)} %get-tuple-element.70, bf16[2048,5632]{1,0:T(8,128)(2,1)} %get-tuple-element.94), kind=kOutput, calls=%fused_computation.38 | convolution fusion | flops 23628087296 | bytes 50331648 | tf_op jit(solution)/shard_map/td,tn->dn/dot_general | solution.py:20
  700.6 16.9 slice_add_fusion.2
  731.8 19.8 %convolution_multiply_fusion.3 = f32[512,5632]{1,0:T(8,128)} fusion(bf16[2048,512]{1,0:T(8,128)(2,1)} %constant_dynamic-update-slice_fusion.2, bf16[2048,5632]{1,0:T(8,128)(2,1)} %get-tuple-element.95), kind=kOutput, calls=%fused_computation.48 | convolution fusion | flops 11814043648 | bytes 36700160 | tf_op jit(solution)/shard_map/td,tn->dn/dot_general | solution.py:20
  752.1 37.0 %convolution_multiply_fusion.1 = f32[1024,5632]{1,0:T(8,128)} fusion(bf16[2048,1024]{1,0:T(8,128)(2,1)} %get-tuple-element.70, bf16[2048,5632]{1,0:T(8,128)(2,1)} %get-tuple-element.95), kind=kOutput, calls=%fused_computation.37 | convolution fusion | flops 23628087296 | bytes 50331648 | tf_op jit(solution)/shard_map/td,tn->dn/dot_general | solution.py:20
  789.2 17.8 slice_add_fusion
  807.0 16.2 slice_add_fusion.1
  823.2 60.6 %fusion.60 = f32[2048,2048]{1,0:T(8,128)} fusion(bf16[2048,5632]{1,0:T(8,128)(2,1)} %get-tuple-element.94, bf16[2048,5632]{1,0:T(8,128)(2,1)} %all-gather.12.cloned.1.call-done), kind=kOutput, calls=%fused_computation.142 | convolution fusion | flops 47244640256 | bytes 62914560 | tf_op jit(solution)/shard_map/tf,df->td/dot_general | solution.py:20
  883.8 69.6 %fusion.10 = (f32[2048]{0:T(1024)}, f32[2048]{0:T(1024)S(1)}, f32[2048,2048]{1,0:T(8,128)}) fusion(bf16[2048,2048]{1,0:T(8,128)(2,1)} %get-tuple-element.161, f32[2048]{0:T(1024)S(1)} %copy-done.18, f32[2048]{0:T(1024)S(1)} %bitcast.123, f32[2048,2048]{1,0:T(8,128)} %fusion.60, bf16[2048,5632]{1,0:T(8,128)(2,1)} %get-tuple-element.95, ...), kind=kOutput, calls=%fused_computation.17 | convolution fusion | flops 47278194688 | bytes 88113152 | tf_op jit(solution)/shard_map/tf,df->td/dot_general | solution.py:20
  969.1 21.2 %convolution_multiply_fusion.6 = f32[2048,2048]{1,0:T(8,128)} fusion(bf16[2048,2048]{1,0:T(8,128)(2,1)S(1)} %copy-done.27, bf16[2048,2048]{1,0:T(8,128)(2,1)S(1)} %fusion.54), kind=kOutput, calls=%fused_computation.51 | convolution fusion | flops 17184063488 | bytes 33554432 | tf_op jit(solution)/shard_map/tn,td->nd/dot_general | solution.py:20
  990.3 23.9 %convolution_convert_fusion.dc_ref = bf16[2048,2048]{1,0:T(8,128)(2,1)} fusion(bf16[2048,2048]{1,0:T(8,128)(2,1)} %copy-done.7, bf16[2048,2048]{1,0:T(8,128)(2,1)} %all-gather.10.cloned.1.call-done), kind=kOutput, calls=%fused_computation.58 | convolution fusion | flops 17184063488 | bytes 25165824 | tf_op jit(solution)/shard_map/td,nd->tn/dot_general | solution.py:20
  1014.2 88.7 %attn_bwd.1 = (bf16[2048,2560]{1,0:T(8,128)(2,1)}, f32[2048,512]{1,0:T(8,128)}, f32[2048,512]{1,0:T(8,128)}) custom-call(bf16[2048,2048]{1,0:T(8,128)(2,1)} %get-tuple-element.67.qb_ref, bf16[2048,2048]{1,0:T(8,128)(2,1)} %convolution_convert_fusion.dc_ref, bf16[2048,512]{1,0:T(8,128)(2,1)S(1)} %rope_kv.1.kv_ref, ...), custom_call_target="tpu_custom_call" | custom-call | flops 10737418240 | bytes 50000000 | tf_op jit(solution)/shard_map/attn_bwd/pallas_call | solution.py:356
  1105.1 24.4 %convolution_multiply_fusion.5 = f32[2048,2048]{1,0:T(8,128)} fusion(bf16[2048,2048]{1,0:T(8,128)(2,1)} %fusion.17, bf16[2048,2560]{1,0:T(8,128)(2,1)} %get-tuple-element.99.wide_ref), kind=kOutput, calls=%fused_computation.50 | convolution fusion | flops 17184063488 | bytes 33554432 | tf_op jit(solution)/shard_map/td,tn->dn/dot_general | solution.py:20
  1129.4 57.2 %fusion.12 = bf16[2048,2048]{1,0:T(8,128)(2,1)} fusion(bf16[2048,2048]{1,0:T(8,128)(2,1)} %get-tuple-element.161, bf16[2048,5632]{1,0:T(8,128)(2,1)} %get-tuple-element.101, bf16[5632,2048]{1,0:T(8,128)(2,1)} %all-gather.16.cloned.1.call-done), kind=kOutput, calls=%fused_computation.19 | convolution fusion | flops 47257223168 | bytes 62914560 | tf_op jit(solution)/shard_map/tf,fd->td/dot_general | solution.py:20
  1213.9 187.1 %collective-permute-done.9 = f32[2,1,704,1024]{3,2,1,0:T(8,128)} collective-permute-done((f32[2,1,704,1024]{3,2,1,0:T(8,128)}, f32[2,1,704,1024]{3,2,1,0:T(8,128)}, u32[]{:S(2)}, u32[]{:S(2)}) %collective-permute-start.9) | collective-permute-done | bytes 5767200 | tf_op jit(solution)/shard_map/ppermute | solution.py:184
  1407.5 193.5 %collective-permute-done.6 = f32[256,5632]{1,0:T(8,128)} collective-permute-done((f32[256,5632]{1,0:T(8,128)}, f32[256,5632]{1,0:T(8,128)}, u32[]{:S(2)}, u32[]{:S(2)}) %collective-permute-start.6) | collective-permute-done | bytes 5767200 | tf_op jit(solution)/shard_map/ppermute | solution.py:184
  1621.2 72.0 %collective-permute-done.7 = f32[128,5632]{1,0:T(8,128)} collective-permute-done((f32[128,5632]{1,0:T(8,128)}, f32[128,5632]{1,0:T(8,128)}, u32[]{:S(2)}, u32[]{:S(2)}) %collective-permute-start.7) | collective-permute-done | bytes 2883616 | tf_op jit(solution)/shard_map/ppermute | solution.py:184
  1701.4 31.8 %fusion.23 = (f32[2048]{0:T(1024)S(1)}, f32[2048]{0:T(1024)S(1)}, f32[2048,2048]{1,0:T(8,128)}) fusion(bf16[32,64,2048]{2,1,0:T(8,128)(2,1)S(1)} %bitcast.103, f32[2048]{0:T(1024)S(1)} %copy-done.21, f32[2048]{0:T(1024)S(1)} %bitcast.127, bf16[2048,2560]{1,0:T(8,128)(2,1)} %unrope_kv.1, bf16[2048,2560]{0,1:T(8,128)(2,1)} %all-gather.8.cloned.1.call-done), kind=kOutput, calls=%fused_computation.33 | convolution fusion | flops 21504192512 | bytes 46170112 | tf_op jit(solution)/shard_map/tn,dn->td/dot_general | solution.py:20
  1733.3 102.1 %all-reduce.1 = f32[8,2,256]{2,1,0:T(2,128)S(1)} all-reduce(f32[8,2,256]{2,1,0:T(2,128)S(1)} %pad_maximum_fusion.6), channel_id=3, replica_groups=mesh['cp'=2,'fsdp'=4] {'fsdp','cp'}, use_global_device_ids=true, to_apply=%region_6.7.clone | all-reduce | flops 4096 | bytes 32768
  1836.7 23.8 %fusion.22 = bf16[2048,2048]{1,0:T(8,128)(2,1)} fusion(bf16[32,64,2048]{2,1,0:T(8,128)(2,1)} %param.12, f32[2048,2048]{1,0:T(8,128)} %get-tuple-element.165, f32[2048]{0:T(1024)S(1)} %broadcast_multiply_fusion, f32[2048]{0:T(1024)S(1)} %bitcast.128, f32[2048]{0:T(1024)S(1)} %copy-done.21, bf16[2048,2048]{1,0:T(8,128)(2,1)} %bitcast.109, ...), kind=kLoop, calls=%fused_computation.32 | loop fusion | flops 67108864 | bytes 67158016 | tf_op jit(solution)/shard_map/convert_element_type | solution.py:386
  (189 shorter events, 222.4 us)
Async XLA Ops:
  7.2 65.7 %all-gather.8.cloned.1.call-start = ((), (), s32[]{:S(2)}) async-start(), calls=%async_computation.6 | async-start | bytes 11796480 | tf_op jit(solution)/shard_map/all_gather | solution.py:171
  9.8 226.6 %all-gather.10.cloned.1.call-start = ((), (), s32[]{:S(2)}) async-start(), calls=%async_computation.7 | async-start | bytes 9437184 | tf_op jit(solution)/shard_map/all_gather | solution.py:171
  10.5 277.3 %all-gather.12.cloned.1.call-start = ((), (), s32[]{:S(2)}) async-start(), calls=%async_computation.8 | async-start | bytes 25952256 | tf_op jit(solution)/shard_map/all_gather | solution.py:171
  11.3 368.1 %all-gather.14.cloned.1.call-start = ((), (), s32[]{:S(2)}) async-start(), calls=%async_computation.9 | async-start | bytes 25952256 | tf_op jit(solution)/shard_map/all_gather | solution.py:171
  11.9 545.7 %all-gather.16.cloned.1.call-start = ((), (), s32[]{:S(2)}) async-start(), calls=%async_computation.10 | async-start | bytes 25952256 | tf_op jit(solution)/shard_map/all_gather | solution.py:171
  30.4 230.6 %copy-start.14 = (f32[8,1,256]{2,1,0:T(1,128)}, f32[8,1,256]{2,1,0:T(1,128)S(1)}, u32[]{:S(2)}) copy-start(f32[8,1,256]{2,1,0:T(1,128)S(1)} %get-tuple-element.153) | copy-start | bytes 24580
  107.4 78.8 %collective-permute-start = (bf16[2048,512]{1,0:T(8,128)(2,1)S(1)}, bf16[2048,512]{1,0:T(8,128)(2,1)}, u32[]{:S(2)}, u32[]{:S(2)}) collective-permute-start(bf16[2048,512]{1,0:T(8,128)(2,1)S(1)} %rope_kv.1.kv_ref), channel_id=1, source_target_pairs={{0,4},{4,0},{1,5},{5,1},{2,6},{6,2},{3,7},{7,3}} | collective-permute-start | bytes 6291464 | tf_op jit(solution)/shard_map/ppermute | solution.py:184
  107.8 1507.2 %reduce-scatter.17.cloned.1.call-start = ((), (), s32[]{:S(2)}) async-start(), calls=%async_computation.16 | async-start | bytes 25952256 | tf_op jit(solution)/shard_map/reduce_scatter | solution.py:175
  108.8 77.5 %copy-start.3 = (f32[256,128]{1,0:T(8,128)}, f32[256,128]{1,0:T(8,128)S(1)}, u32[]{:S(2)}) copy-start(f32[256,128]{1,0:T(8,128)S(1)} %maximum_maximum_fusion.1.sin_ref) | copy-start | bytes 393220
  474.8 50.6 %collective-permute-start.1 = (f32[2816,1024]{1,0:T(8,128)}, f32[2816,1024]{1,0:T(8,128)}, u32[]{:S(2)}, u32[]{:S(2)}) collective-permute-start(f32[2816,1024]{1,0:T(8,128)} %fusion.37), channel_id=1, source_target_pairs={{0,1},{1,0},{2,3},{3,2},{4,5},{5,4},{6,7},{7,6}} | collective-permute-start | bytes 34603016 | tf_op jit(solution)/shard_map/ppermute | solution.py:184
  512.4 1353.7 %reduce-scatter.13.cloned.1.call-start = ((), (), s32[]{:S(2)}) async-start(), calls=%async_computation.14 | async-start | bytes 25952256 | tf_op jit(solution)/shard_map/reduce_scatter | solution.py:175
  663.7 36.9 %collective-permute-start.2 = (f32[512,5632]{1,0:T(8,128)}, f32[512,5632]{1,0:T(8,128)}, u32[]{:S(2)}, u32[]{:S(2)}) collective-permute-start(f32[512,5632]{1,0:T(8,128)} %convolution_multiply_fusion.4), channel_id=1, source_target_pairs={{0,1},{1,0},{2,3},{3,2},{4,5},{5,4},{6,7},{7,6}} | collective-permute-start | bytes 34603016 | tf_op jit(solution)/shard_map/ppermute | solution.py:184
  751.6 37.6 %collective-permute-start.3 = (f32[512,5632]{1,0:T(8,128)}, f32[512,5632]{1,0:T(8,128)}, u32[]{:S(2)}, u32[]{:S(2)}) collective-permute-start(f32[512,5632]{1,0:T(8,128)} %convolution_multiply_fusion.3), channel_id=1, source_target_pairs={{0,1},{1,0},{2,3},{3,2},{4,5},{5,4},{6,7},{7,6}} | collective-permute-start | bytes 34603016 | tf_op jit(solution)/shard_map/ppermute | solution.py:184
  752.1 1119.6 %reduce-scatter.9.cloned.1.call-start = ((), (), s32[]{:S(2)}) async-start(), calls=%async_computation.12 | async-start | bytes 4718592 | tf_op jit(solution)/shard_map/reduce_scatter | solution.py:175
  823.2 363.4 %collective-permute-start.4 = (f32[256,5632]{1,0:T(8,128)}, f32[256,5632]{1,0:T(8,128)}, u32[]{:S(2)}, u32[]{:S(2)}) collective-permute-start(f32[256,5632]{1,0:T(8,128)} %slice_add_fusion.1), channel_id=1, source_target_pairs={{0,4},{4,0},{1,5},{5,1},{2,6},{6,2},{3,7},{7,3}} | collective-permute-start | bytes 17301512 | tf_op jit(solution)/shard_map/ppermute | solution.py:184
  1102.8 92.4 %collective-permute-start.5 = (f32[2048,512]{1,0:T(8,128)}, f32[2048,512]{1,0:T(8,128)}, u32[]{:S(2)}, u32[]{:S(2)}) collective-permute-start(f32[2048,512]{1,0:T(8,128)} %get-tuple-element.108), channel_id=1, source_target_pairs={{0,4},{4,0},{1,5},{5,1},{2,6},{6,2},{3,7},{7,3}} | collective-permute-start | bytes 12582920 | tf_op jit(solution)/shard_map/ppermute | solution.py:184
  1209.8 664.7 %reduce-scatter.15.cloned.1.call-start = ((), (), s32[]{:S(2)}) async-start(), calls=%async_computation.15 | async-start | bytes 25952256 | tf_op jit(solution)/shard_map/reduce_scatter | solution.py:175
  1210.5 669.5 %reduce-scatter.7.cloned.1.call-start = ((), (), s32[]{:S(2)}) async-start(), calls=%async_computation.11 | async-start | bytes 18874368 | tf_op jit(solution)/shard_map/reduce_scatter | solution.py:175
  1211.1 671.8 %reduce-scatter.11.cloned.1.call-start = ((), (), s32[]{:S(2)}) async-start(), calls=%async_computation.13 | async-start | bytes 18874368 | tf_op jit(solution)/shard_map/reduce_scatter | solution.py:175
  1211.8 189.1 %collective-permute-start.9 = (f32[2,1,704,1024]{3,2,1,0:T(8,128)}, f32[2,1,704,1024]{3,2,1,0:T(8,128)}, u32[]{:S(2)}, u32[]{:S(2)}) collective-permute-start(f32[2,1,704,1024]{3,2,1,0:T(8,128)} %constant_dynamic-slice_fusion), channel_id=1, source_target_pairs={{0,4},{4,0},{1,5},{5,1},{2,6},{6,2},{3,7},{7,3}} | collective-permute-start | bytes 17301512 | tf_op jit(solution)/shard_map/ppermute | solution.py:184
  1213.6 387.4 %collective-permute-start.6 = (f32[256,5632]{1,0:T(8,128)}, f32[256,5632]{1,0:T(8,128)}, u32[]{:S(2)}, u32[]{:S(2)}) collective-permute-start(f32[256,5632]{1,0:T(8,128)} %slice_add_fusion.3), channel_id=1, source_target_pairs={{0,4},{4,0},{1,5},{5,1},{2,6},{6,2},{3,7},{7,3}} | collective-permute-start | bytes 17301512 | tf_op jit(solution)/shard_map/ppermute | solution.py:184
  1213.9 394.0 %copy-start.31 = (u32[8]{0:T(128)S(1)}, u32[8]{0:T(128)}, u32[]{:S(2)}) copy-start(u32[8]{0:T(128)} %constant.169) | copy-start | bytes 100
  1406.1 202.4 %collective-permute-start.10 = (f32[1,704,1024]{2,1,0:T(8,128)}, f32[1,704,1024]{2,1,0:T(8,128)}, u32[]{:S(2)}, u32[]{:S(2)}) collective-permute-start(f32[1,704,1024]{2,1,0:T(8,128)} %fusion.43), channel_id=1, source_target_pairs={{0,2},{2,0},{1,3},{3,1},{4,6},{6,4},{5,7},{7,5}} | collective-permute-start | bytes 8650760 | tf_op jit(solution)/shard_map/ppermute | solution.py:184
  1605.9 87.3 %collective-permute-start.7 = (f32[128,5632]{1,0:T(8,128)}, f32[128,5632]{1,0:T(8,128)}, u32[]{:S(2)}, u32[]{:S(2)}) collective-permute-start(f32[128,5632]{1,0:T(8,128)} %slice_add_fusion.7), channel_id=1, source_target_pairs={{0,2},{2,0},{1,3},{3,1},{4,6},{6,4},{5,7},{7,5}} | collective-permute-start | bytes 8650760 | tf_op jit(solution)/shard_map/ppermute | solution.py:184
  1615.0 86.5 %slice-start = ((s8[8388608]{0:T(1024)(128)(4,1)}), s8[4194304]{0:T(1024)(128)(4,1)S(1)}, s32[]{:S(2)}) async-start(s8[8388608]{0:T(1024)(128)(4,1)} %bitcast.102), calls=%async_computation.17 | async-start | bytes 8388608
  1621.2 80.2 %slice-start.1 = ((s8[8388608]{0:T(1024)(128)(4,1)}), s8[4194304]{0:T(1024)(128)(4,1)S(1)}, s32[]{:S(2)}) async-start(s8[8388608]{0:T(1024)(128)(4,1)} %bitcast.102), calls=%async_computation.18 | async-start | bytes 8388608
  1621.2 80.2 %copy-start.21 = (f32[2048]{0:T(1024)S(1)}, f32[2048]{0:T(1024)}, u32[]{:S(2)}) copy-start(f32[2048]{0:T(1024)} %copy-done.20) | copy-start | bytes 24580
  1621.2 80.2 %copy-start.23 = (f32[8,1,256]{2,1,0:T(1,128)S(1)}, f32[8,1,256]{2,1,0:T(1,128)}, u32[]{:S(2)}) copy-start(f32[8,1,256]{2,1,0:T(1,128)} %copy-done.22) | copy-start | bytes 24580
  1700.0 136.7 %copy-start.16 = (f32[8,1,256]{2,1,0:T(1,128)S(1)}, f32[8,1,256]{2,1,0:T(1,128)}, u32[]{:S(2)}) copy-start(f32[8,1,256]{2,1,0:T(1,128)} %copy-done.14) | copy-start | bytes 24580
  1700.0 136.7 %copy-start.19 = (f32[2048]{0:T(1024)S(1)}, f32[2048]{0:T(1024)}, u32[]{:S(2)}) copy-start(f32[2048]{0:T(1024)} %copy-done.17) | copy-start | bytes 24580
  1700.0 136.7 %copy-start.25 = (f32[2048]{0:T(1024)S(1)}, f32[2048]{0:T(1024)}, u32[]{:S(2)}) copy-start(f32[2048]{0:T(1024)} %copy-done.24) | copy-start | bytes 24580
  1700.0 160.5 %collective-permute-start.8 = (f32[128,5632]{1,0:T(8,128)}, f32[128,5632]{1,0:T(8,128)}, u32[]{:S(2)}, u32[]{:S(2)}) collective-permute-start(f32[128,5632]{1,0:T(8,128)} %slice_add_fusion.9), channel_id=1, source_target_pairs={{0,2},{2,0},{1,3},{3,1},{4,6},{6,4},{5,7},{7,5}} | collective-permute-start | bytes 8650760 | tf_op jit(solution)/shard_map/ppermute | solution.py:184
  (26 other events, 544.5 us)
Sparse Core Ops, SparseCore 0:
  10.4 62.4 all-gather.7
  74.7 59.9 all-gather.9
  136.5 130.3 all-gather.11
  268.6 110.7 all-gather.13
  381.0 112.2 all-gather.15
  512.5 137.8 reduce-scatter.16
  752.2 204.4 reduce-scatter.12
  1209.9 61.1 reduce-scatter.8
  1274.7 230.8 reduce-scatter.14
  1508.9 160.1 reduce-scatter.6
  1673.2 158.4 reduce-scatter.10
